TPU v7x, 32 devices: a whole 2x2x4 slice. The times are simulated.
32 devices in a mesh: band: 4 (over z), px: 4 (over x, core), py: 2 (over y).
Axes of the slice: x: 2, y: 2, z: 4, core: 2. Of those that a mesh axis runs over, the one named last changes fastest.
Arguments:
- orbitals: bfloat16 [4, 1024, 384], P('band', ('px', 'py')), may hold values from -0.01171875 to 0.01171875
- occupations: float32 [4], P('band'), may hold values from 0.2 to 2
- stick_map: int32 [2, 1024], P(None, 'px'), may hold values from 0 to 191, as said below
- core_density: float32 [192, 192, 192], P('py', 'px'), may hold values from 0.05 to 0.5
Outputs:
- potential: float32 [192, 192, 192], P('py', 'px')
- gradient: float32 [3, 192, 192, 192], P(None, 'py', 'px')
Inputs may be any that keep to these rules, and one draw needn't show every extreme that they name: `stick_map`: columns i * 128 * 2 to (i + 1) * 128 * 2 - 1 have x index from i * 48 to (i + 1) * 48 - 1; no two columns share a grid position.
All inputs are finite; a program needn't handle non-finite values.
Results may differ from a plain program's by a relative error of at most 0.0054.
Values may be sent and summed in bfloat16 or wider, within the bound.
No kernel may reach another device: no remote copies, remote signals or barrier semaphores. Data moves between devices by JAX's collectives and lax.ppermute only.
A program may use at most 128 MiB of HBM per device.

v0:
```python
import math

import jax
import jax.numpy as jnp
from jax import lax
from jax.sharding import PartitionSpec as P

SPACING = 0.25
PBE_KAPPA = 0.804
PBE_MU = 0.2195
SLATER_COEF = 0.75 * (3.0 / math.pi) ** (1.0 / 3.0)
REDUCED_SCALE = 4.0 * (3.0 * math.pi**2) ** (2.0 / 3.0)
HIGHEST_PREC = lax.Precision.HIGHEST


def complex_table(row_index, col_index, points, direction):
    product = row_index[:, None] * col_index[None, :] % points
    angles = 2.0 * math.pi / points * product.astype(jnp.float32)
    cosine = jnp.cos(angles)
    sine_part = direction * jnp.sin(angles)
    return jnp.stack([jnp.stack([cosine, sine_part], 1), jnp.stack([-sine_part, cosine], 1)], 0)


def freq_pair(positions, points):
    signed = jnp.where(positions <= points // 2, positions, positions - points).astype(jnp.float32)
    gradient_freq = jnp.where(positions == points // 2, 0.0, signed)
    return (signed, gradient_freq)


def swap_rows(values):
    return lax.all_to_all(values, "px", split_axis=1, concat_axis=0, tiled=True)


def swap_depth(values):
    moved = lax.all_to_all(values, ("band", "py"), split_axis=1, concat_axis=0, tiled=True)
    return moved


def exchange_part(density, fields):
    cube_root = jnp.cbrt(density)
    four_thirds = density * cube_root
    grad_square = fields[1] * fields[1] + fields[2] * fields[2] + fields[3] * fields[3]
    reduced = grad_square / (REDUCED_SCALE * four_thirds * four_thirds)
    denominator = 1.0 + PBE_MU * reduced / PBE_KAPPA
    enhance = 1.0 + PBE_KAPPA - PBE_KAPPA / denominator
    enhance_slope = PBE_MU / (denominator * denominator)
    potential = fields[0] - SLATER_COEF * cube_root * (
        4.0 / 3.0 * enhance - 8.0 / 3.0 * reduced * enhance_slope
    )
    return jnp.concatenate([potential[None], fields[1:]], 0)


def transform(rho_local, pieces, depth_index, px_index):
    zshare, y_rows, points = rho_local.shape
    rows_px = lax.axis_size("px")
    rows_py = lax.axis_size("py")
    xblock = points // rows_px
    kyblock = points // pieces
    zblock = zshare * (pieces // rows_py)
    every_index = jnp.arange(points, dtype=jnp.int32)
    forward = complex_table(every_index, every_index, points, -1.0)
    x_table = forward[0].reshape(points, 2, rows_px, xblock).transpose(0, 2, 1, 3)
    section_data = jnp.einsum("zyx,xbsk->ybzsk", rho_local, x_table, precision=HIGHEST_PREC)
    section_data = swap_rows(section_data.reshape(y_rows, rows_px, zshare * 2 * xblock))
    section_data = section_data.reshape(points, zshare, 2, xblock)
    y_table = forward.reshape(2, points, 2, pieces, kyblock)
    section_data = jnp.einsum("yzrx,rysdk->zdksx", section_data, y_table, precision=HIGHEST_PREC)
    section_data = swap_depth(section_data.reshape(zshare, pieces, kyblock * 2 * xblock))
    section_data = section_data.reshape(pieces * zshare, kyblock, 2, xblock)
    source = jnp.arange(pieces * zshare, dtype=jnp.int32)
    device = source // zshare
    within = source % zshare
    z_order = device % rows_py * zblock + device // rows_py * zshare + within
    z_table = complex_table(z_order, every_index, points, -1.0)
    spectrum = jnp.einsum("zyrx,rzsk->kysx", section_data, z_table, precision=HIGHEST_PREC)
    q_depth, g_depth = freq_pair(every_index, points)
    ky_index = depth_index * kyblock + jnp.arange(kyblock, dtype=jnp.int32)
    q_col, g_col = freq_pair(ky_index, points)
    kx_index = px_index * xblock + jnp.arange(xblock, dtype=jnp.int32)
    q_row, g_row = freq_pair(kx_index, points)
    wave_unit = 2.0 * math.pi / (points * SPACING)
    squared = wave_unit**2 * (
        q_depth[:, None, None] ** 2 + q_col[None, :, None] ** 2 + q_row[None, None, :] ** 2
    )
    hartree = jnp.where(squared > 0, 4.0 * math.pi / jnp.where(squared > 0, squared, 1.0), 0.0)
    wave_z = wave_unit * g_depth[:, None, None]
    wave_y = wave_unit * g_col[None, :, None]
    wave_x = wave_unit * g_row[None, None, :]
    real_part = spectrum[:, :, 0, :]
    imag_part = spectrum[:, :, 1, :]
    first_factor = hartree - wave_x
    packed = jnp.stack(
        [
            jnp.stack([first_factor * real_part, first_factor * imag_part], 2),
            jnp.stack(
                [-wave_z * real_part - wave_y * imag_part, wave_y * real_part - wave_z * imag_part],
                2,
            ),
        ],
        0,
    )
    inverse = complex_table(every_index, every_index, points, 1.0)
    zi_table = complex_table(every_index, z_order, points, 1.0).reshape(
        2, points, 2, pieces, zshare
    )
    section_data = jnp.einsum("fkyrx,rksdz->ydfzsx", packed, zi_table, precision=HIGHEST_PREC)
    section_data = swap_depth(section_data.reshape(kyblock, pieces, 2 * zshare * 2 * xblock))
    section_data = section_data.reshape(points, 2, zshare, 2, xblock)
    yi_table = inverse.reshape(2, points, 2, rows_px, y_rows)
    section_data = jnp.einsum("kfzrx,rksby->xbfzsy", section_data, yi_table, precision=HIGHEST_PREC)
    section_data = swap_rows(section_data.reshape(xblock, rows_px, 2 * zshare * 2 * y_rows))
    section_data = section_data.reshape(points, 2, zshare, 2, y_rows)
    fields = jnp.einsum("kfzry,rksx->fszyx", section_data, inverse, precision=HIGHEST_PREC)
    fields = fields * (1.0 / float(points) ** 3)
    return fields.reshape(4, zshare, y_rows, points)


def body(orbitals, occupations, stick_map, core_density):
    bands_here, columns_here, doubled = orbitals.shape
    points = doubled // 2
    rows_px = lax.axis_size("px")
    rows_py = lax.axis_size("py")
    groups = lax.axis_size("band")
    px_index = lax.axis_index("px")
    py_index = lax.axis_index("py")
    xblock = points // rows_px
    zblock = points // rows_py
    y_rows = points // rows_px
    every_index = jnp.arange(points, dtype=jnp.int32)
    inverse = complex_table(every_index, every_index, points, 1.0)
    z_table = (
        inverse.reshape(2, points, 2, rows_py, zblock)
        .transpose(0, 1, 3, 2, 4)
        .reshape(doubled, doubled)
    )
    columns = jnp.dot(
        orbitals.astype(jnp.float32).reshape(bands_here * columns_here, doubled),
        z_table,
        precision=HIGHEST_PREC,
    )
    columns = columns.astype(jnp.bfloat16).reshape(bands_here, columns_here, doubled)
    columns = lax.all_to_all(columns, "py", split_axis=2, concat_axis=1, tiled=True)
    slot_index = stick_map[1] * xblock + (stick_map[0] - px_index * xblock)
    plane_data = (
        jnp.zeros((bands_here, points * xblock, 2 * zblock), jnp.float32)
        .at[:, slot_index]
        .set(columns.astype(jnp.float32))
    )
    plane_data = plane_data.reshape(bands_here, points, xblock, 2, zblock)
    plane_data = jnp.einsum("byxrz,rysk->bkxsz", plane_data, inverse, precision=HIGHEST_PREC)
    plane_data = plane_data.astype(jnp.bfloat16).reshape(bands_here, points, xblock * 2 * zblock)
    plane_data = lax.all_to_all(plane_data, "px", split_axis=1, concat_axis=2, tiled=True)
    plane_data = plane_data.astype(jnp.float32).reshape(bands_here, y_rows, points, 2, zblock)
    orbital_values = jnp.einsum("byxrz,rxsk->bszyk", plane_data, inverse, precision=HIGHEST_PREC)
    density = jnp.einsum(
        "b,bszyk->zyk", occupations, orbital_values * orbital_values, precision=HIGHEST_PREC
    )
    zshare = zblock // groups
    band_index = lax.axis_index("band")
    shared_rows = lax.psum_scatter(density, "band", scatter_dimension=0, tiled=True)
    core_rows = lax.dynamic_slice_in_dim(core_density, band_index * zshare, zshare, 0)
    rho_local = shared_rows + core_rows
    fields = transform(rho_local, groups * rows_py, band_index * rows_py + py_index, px_index)
    results = lax.all_gather(exchange_part(rho_local, fields), "band", axis=1, tiled=True)
    return (results[0], results[1:4])


def solution(mesh):
    return jax.shard_map(
        body,
        mesh=mesh,
        in_specs=(P("band", ("px", "py"), None), P("band"), P(None, "px"), P("py", "px", None)),
        out_specs=(P("py", "px", None), P(None, "py", "px", None)),
        check_vma=False,
    )
```

profile of v0, /device:TPU:0, one launch (start us, length us, event | category | flops | bytes accessed | tf_op | source)
XLA Modules:
  0.0 1160.9 jit_solution(13728535052132577211)
XLA Ops:
  27.8 12.3 %reshape.807 = f32[192,48,2,96]{3,2,1,0:T(2,128)} reshape(f32[9216,192]{1,0:T(8,128)} %scatter_custom_fusion) | data formatting | bytes 14155776 | tf_op jit(solution)/shard_map/reshape.2
  40.1 14.2 %copy.140 = f32[192,48,2,96]{0,3,2,1:T(8,128)} copy(f32[192,48,2,96]{3,2,1,0:T(2,128)} %reshape.807) | data formatting | bytes 14155776 | tf_op jit(solution)/shard_map/reshape.2
  54.3 18.6 %fusion.5 = bf16[1,192,48,2,96]{1,4,2,3,0:T(8,128)(2,1)} fusion(f32[192,48,2,96]{0,3,2,1:T(8,128)} %copy.140, f32[1,192,2,192]{3,1,0,2:T(8,128)S(1)} %get-tuple-element.11, f32[1,192,2,192]{3,1,0,2:T(8,128)S(1)} %get-tuple-element.10), kind=kOutput, calls=%fused_computation.8 | convolution fusion | flops 8155643904 | bytes 11206656 | tf_op jit(solution)/shard_map/byxrz,rysk->bkxsz/dot_general | solution.py:150
  72.8 11.6 copy.141
  84.4 24.4 %reshape.857 = bf16[1,192,9216]{2,0,1:T(2,128)(2,1)} reshape(bf16[1,192,48,2,96]{4,3,2,1,0:T(2,128)(2,1)} %copy.141) | data formatting | bytes 7077888 | tf_op jit(solution)/shard_map/reshape | solution.py:151
  108.8 78.5 %reduce.4 = bf16[192,9216]{1,0:T(8,128)(2,1)} reduce(bf16[192,1,9216]{2,1,0:T(2,128)(2,1)} %bitcast.221, bf16[]{:T(256)} %broadcast.1309), dimensions={1}, to_apply=%bitcast.207.reduce_sub_computation | reduce | bytes 7077890
  198.3 40.5 %all-to-all-done.1 = bf16[4,2,221184]{2,1,0:T(2,128)(2,1)} async-done(((bf16[4,2,221184]{2,1,0:T(2,128)(2,1)}), bf16[4,2,221184]{2,1,0:T(2,128)(2,1)}, u32[]{:S(2)}, u32[]{:S(2)}) %all-to-all-start.1) | async-done | bytes 3538976 | tf_op jit(solution)/shard_map/all_to_all | solution.py:152
  254.0 14.9 %reshape.809 = bf16[48,192,2,96]{3,2,1,0:T(2,128)(2,1)} reshape(bf16[1,48,4,9216]{3,2,1,0:T(4,128)(2,1)} %copy.143) | data formatting | bytes 7077888 | tf_op jit(solution)/shard_map/reshape.5
  268.9 10.5 fusion.2
  289.7 84.4 %reduce-scatter.2.cloned.1.call-done = f32[24,48,192]{2,1,0:T(8,128)} async-done(((f32[96,48,192]{2,1,0:T(8,128)}), f32[24,48,192]{2,1,0:T(8,128)}) %reduce-scatter.2.cloned.1.call-update) | async-done | bytes 884752 | tf_op jit(solution)/shard_map/reduce_scatter | solution.py:160
  402.4 21.2 %all-to-all-done.2 = f32[48,4,2304]{2,0,1:T(8,128)S(1)} async-done(((f32[48,4,2304]{2,0,1:T(8,128)}), f32[48,4,2304]{2,0,1:T(8,128)S(1)}, u32[]{:S(2)}, u32[]{:S(2)}) %all-to-all-start.2) | async-done | bytes 1769504 | tf_op jit(solution)/shard_map/all_to_all | solution.py:31
  466.9 37.3 %all-to-all-done.3 = f32[24,8,2304]{2,0,1:T(8,128)S(1)} async-done(((f32[24,8,2304]{2,0,1:T(8,128)}), f32[24,8,2304]{2,0,1:T(8,128)S(1)}, u32[]{:S(2)}, u32[]{:S(2)}) %all-to-all-start.3) | async-done | bytes 1769504 | tf_op jit(solution)/shard_map/all_to_all | solution.py:35
  525.6 15.9 %fusion.22 = f32[24,8,2,24,2,48]{5,3,0,2,1,4:T(8,128)S(1)} fusion(f32[1,192,24,2,48]{1,4,2,3,0:T(8,128)S(1)} %maximum_bitcast_fusion.5, f32[1,192,24,2,48]{1,4,2,3,0:T(8,128)S(1)} %maximum_bitcast_fusion.4, f32[1,192,1,8,24]{1,4,0,3,2:T(8,128)S(1)} %copy-done.4, f32[1,192,1,8,24]{1,4,0,3,2:T(8,128)S(1)} %copy-done.3, ...), kind=kOutput, calls=%fused_computation.28 | convolution fusion | flops 4078190592 | bytes 7520256 | tf_op jit(solution)/shard_map/fkyrx,rksdz->ydfzsx/dot_general | solution.py:106
  549.5 16.6 %reshape.859 = f32[24,8,4608]{2,0,1:T(8,128)} reshape(f32[24,8,2,24,2,48]{5,4,3,2,0,1:T(2,128)} %copy.189) | data formatting | bytes 7077888 | tf_op jit(solution)/shard_map/reshape | solution.py:107
  571.5 77.6 %all-to-all-done.4 = f32[24,8,4608]{2,0,1:T(8,128)} async-done(((f32[24,8,4608]{2,0,1:T(8,128)}), f32[24,8,4608]{2,0,1:T(8,128)}, u32[]{:S(2)}, u32[]{:S(2)}) %all-to-all-start.4) | async-done | bytes 3538976 | tf_op jit(solution)/shard_map/all_to_all | solution.py:35
  649.2 17.3 %reshape.816 = f32[192,2,24,2,48]{4,3,2,1,0:T(2,128)} reshape(f32[8,24,1,4608]{3,1,0,2:T(8,128)} %bitcast.63) | data formatting | bytes 7077888 | tf_op jit(solution)/shard_map/reshape | solution.py:108
  666.5 24.9 %fusion.19 = f32[48,4,2,24,2,48]{0,5,3,2,1,4:T(8,128)} fusion(f32[192,2,24,2,48,1,1]{4,3,2,1,0,6,5:T(2,128)} %bitcast.218, f32[1,192,1,4,48]{1,4,0,3,2:T(8,128)S(1)} %get-tuple-element.20, f32[1,192,1,4,48]{1,4,0,3,2:T(8,128)S(1)} %get-tuple-element.19, f32[1,192,1,4,48]{1,4,0,3,2:T(8,128)S(1)} %get-tuple-element.18), kind=kOutput, calls=%fused_computation.27 | convolution fusion | flops 4077305856 | bytes 7520256 | tf_op jit(solution)/shard_map/kfzrx,rksby->xbfzsy/dot_general | solution.py:110
  691.4 13.7 %copy.157 = f32[48,4,2,24,2,48]{5,4,3,2,0,1:T(2,128)} copy(f32[48,4,2,24,2,48]{0,5,3,2,1,4:T(8,128)} %fusion.19) | data formatting | bytes 7077888 | tf_op jit(solution)/shard_map/kfzrx,rksby->xbfzsy/transpose | solution.py:110
  705.1 16.6 %reshape.817 = f32[48,4,4608]{2,0,1:T(8,128)} reshape(f32[48,4,2,24,2,48]{5,4,3,2,0,1:T(2,128)} %copy.157) | data formatting | bytes 7077888 | tf_op jit(solution)/shard_map/reshape | solution.py:111
  721.7 46.9 %all_to_all.84 = f32[48,4,4608]{2,0,1:T(8,128)} all-to-all(f32[48,4,4608]{2,0,1:T(8,128)} %reshape.817), channel_id=1, replica_groups=mesh['band'=4,'px'=4,'py'=2] {'px'}, dimensions={1} | all-to-all | bytes 7077888 | tf_op jit(solution)/shard_map/all_to_all | solution.py:31
  768.6 17.1 %reshape.818 = f32[192,2,24,2,48]{4,3,2,1,0:T(2,128)} reshape(f32[4,48,1,4608]{3,1,0,2:T(8,128)} %bitcast.224) | data formatting | bytes 7077888 | tf_op jit(solution)/shard_map/reshape | solution.py:112
  785.7 13.2 %copy.158 = f32[192,2,24,2,48]{0,4,3,2,1:T(8,128)} copy(f32[192,2,24,2,48]{4,3,2,1,0:T(2,128)} %reshape.818) | data formatting | bytes 7077888 | tf_op jit(solution)/shard_map/reshape | solution.py:112
  816.6 320.4 %all-gather.2.cloned.1.call-done = f32[4,96,48,192]{3,2,1,0:T(8,128)} async-done(((f32[4,24,48,192]{3,2,1,0:T(8,128)}), f32[4,96,48,192]{3,2,1,0:T(8,128)}) %all-gather.2.cloned.1.call-update) | async-done | bytes 14155792 | tf_op jit(solution)/shard_map/all_gather | solution.py:164
  1141.8 11.8 %slice.55 = f32[3,96,48,192]{3,2,1,0:T(8,128)} slice(f32[4,96,48,192]{3,2,1,0:T(8,128)} %all-gather.2.cloned.1.call-done), slice={[1:4], [0:96], [0:48], [0:192]} | slice | bytes 21233664 | tf_op jit(solution)/shard_map/slice | solution.py:165
  (82 shorter events, 185.1 us)
Async XLA Ops:
  7.2 2.2 copy-start
  8.1 10.4 copy-start.5
  12.6 8.6 all-to-all-start
  192.9 45.9 %all-to-all-start.1 = ((bf16[4,2,221184]{2,1,0:T(2,128)(2,1)}), bf16[4,2,221184]{2,1,0:T(2,128)(2,1)}, u32[]{:S(2)}, u32[]{:S(2)}) async-start(bf16[4,2,221184]{2,1,0:T(2,128)(2,1)} %reshape.864), calls=%async_computation.1 | async-start | bytes 7077888 | tf_op jit(solution)/shard_map/all_to_all | solution.py:152
  197.6 176.5 %reduce-scatter.2.cloned.1.call-start = ((), (), s32[]{:S(2)}) async-start(), calls=%async_computation.7 | async-start | bytes 5898240 | tf_op jit(solution)/shard_map/reduce_scatter | solution.py:160
  397.7 25.9 %all-to-all-start.2 = ((f32[48,4,2304]{2,0,1:T(8,128)}), f32[48,4,2304]{2,0,1:T(8,128)S(1)}, u32[]{:S(2)}, u32[]{:S(2)}) async-start(f32[48,4,2304]{2,0,1:T(8,128)} %reshape.811), calls=%async_computation.3 | async-start | bytes 3538944 | tf_op jit(solution)/shard_map/all_to_all | solution.py:31
  458.1 46.0 %all-to-all-start.3 = ((f32[24,8,2304]{2,0,1:T(8,128)}), f32[24,8,2304]{2,0,1:T(8,128)S(1)}, u32[]{:S(2)}, u32[]{:S(2)}) async-start(f32[24,8,2304]{2,0,1:T(8,128)} %reshape.858), calls=%async_computation.4 | async-start | bytes 3538944 | tf_op jit(solution)/shard_map/all_to_all | solution.py:35
  524.6 0.9 copy-start.3
  524.6 1.0 copy-start.4
  566.1 83.1 %all-to-all-start.4 = ((f32[24,8,4608]{2,0,1:T(8,128)}), f32[24,8,4608]{2,0,1:T(8,128)}, u32[]{:S(2)}, u32[]{:S(2)}) async-start(f32[24,8,4608]{2,0,1:T(8,128)} %reshape.859), calls=%async_computation.5 | async-start | bytes 7077888 | tf_op jit(solution)/shard_map/all_to_all | solution.py:35
  570.6 566.4 %all-gather.2.cloned.1.call-start = ((), (), s32[]{:S(2)}) async-start(), calls=%async_computation.8 | async-start | bytes 23592960 | tf_op jit(solution)/shard_map/all_gather | solution.py:164
  809.6 1.3 copy-start.2
  1141.8 11.8 %copy-start.1 = (bf16[1,128,384]{2,1,0:T(8,128)(2,1)S(1)}, bf16[1,128,384]{2,1,0:T(8,128)(2,1)}, u32[]{:S(2)}) copy-start(bf16[1,128,384]{2,1,0:T(8,128)(2,1)} %param.4) | copy-start | bytes 294916
Sparse Core Ops, SparseCore 0:
  288.9 85.1 reduce-scatter.1
  816.7 320.2 all-gather.1
where the time goes:
time: 1170 us; the launch traced here: 1160 us
  waiting for transfers between devices  584 us (50%)
  local copies, waits for them, and re-layouts  291 us (25%)
  matrix products  103 us (9%)
  other arithmetic  98.1 us (8%)
  blocking collectives  46.9 us (4%)
  starting transfers between devices  22.4 us (2%)
  between operations  15.5 us (1%)
    all_gather x1, waiting for transfers between devices, body(): lax.all_gather(exchange_part(rho_local, fields), 'band', axis=1, tiled=True)  320 us
    all_to_all x2, waiting for transfers between devices, swap_depth(): lax.all_to_all(values, ('band', 'py'), split_axis=1, concat_axis=0, tiled...  115 us
    reduce_scatter x1, waiting for transfers between devices, body(): lax.psum_scatter(density, 'band', scatter_dimension=0, tiled=True)  84.4 us
    unnamed x2, other arithmetic  79.7 us
    all_to_all x1, blocking collectives, swap_rows(): return lax.all_to_all(values, 'px', split_axis=1, concat_axis=0, tiled=True)  46.9 us
    another operation x3, local copies, waits for them, and re-layouts  41.4 us
    all_to_all x1, waiting for transfers between devices, body(): lax.all_to_all(plane_data, 'px', split_axis=1, concat_axis=2, tiled=True)  40.5 us
    reshape x2, local copies, waits for them, and re-layouts, transform(): section_data = section_data.reshape(points, 2, zshare, 2, y_rows)  30.3 us
  transfers between devices with their start and end apart: 7, of which 7 were waited for; matrix products, arithmetic and copies ran while one was open for 1% of the time, Pallas kernels for 0%

commit v1 on v0

--- a/solution.py
+++ b/solution.py
@@ -2,7 +2,10 @@
 
 import jax
 import jax.numpy as jnp
+import numpy as np
 from jax import lax
+from jax.experimental import pallas as pl
+from jax.experimental.pallas import tpu as pltpu
 from jax.sharding import PartitionSpec as P
 
 SPACING = 0.25
@@ -115,7 +118,7 @@
     return fields.reshape(4, zshare, y_rows, points)
 
 
-def body(orbitals, occupations, stick_map, core_density):
+def pencil_body(orbitals, occupations, stick_map, core_density):
     bands_here, columns_here, doubled = orbitals.shape
     points = doubled // 2
     rows_px = lax.axis_size("px")
@@ -165,6 +168,429 @@
     return (results[0], results[1:4])
 
 
+AXES = ("band", "px", "py")
+ROW_PAD = 8
+LANES = 128
+BF16 = jnp.bfloat16
+F32 = jnp.float32
+LANE_DOT = (((1,), (1,)), ((), ()))
+
+
+def split_table(table):
+    high = table.astype(BF16)
+    low = (table - high.astype(np.float64)).astype(BF16)
+    return high, low
+
+
+def wave_tables(points):
+    steps = np.arange(points)
+    angles = 2.0 * np.pi / points * ((steps[:, None] * steps[None, :]) % points)
+    return np.cos(angles), np.sin(angles)
+
+
+def real_basis(points):
+    cosine, sine = wave_tables(points)
+    half = points // 2
+    rows = np.where(np.arange(points)[:, None] <= half, cosine, sine)
+    scale = np.full((points, 1), np.sqrt(2.0 / points))
+    scale[0] = scale[half] = np.sqrt(1.0 / points)
+    return rows * scale
+
+
+def derivative(points):
+    _, sine = wave_tables(points)
+    half = points // 2
+    freq = np.arange(points)
+    freq = np.where(freq < half, freq, freq - points).astype(np.float64)
+    freq[half] = 0.0
+    unit = 2.0 * np.pi / (points * SPACING)
+    column = -(unit / points) * (freq[:, None] * sine).sum(0)
+    steps = np.arange(points)
+    return column[(steps[:, None] - steps[None, :]) % points]
+
+
+def left3(table):
+    high, low = split_table(table)
+    return np.concatenate([high, high, low], 1)
+
+
+def right3(table):
+    high, low = split_table(table)
+    return np.concatenate([high, high, low], 0)
+
+
+def two_parts(values):
+    high = values.astype(BF16)
+    return high, (values - high.astype(F32)).astype(BF16)
+
+
+def mul_left(table3, values):
+    high, low = two_parts(values)
+    return jnp.dot(table3, jnp.concatenate([high, low, high], 0), preferred_element_type=F32)
+
+
+def mul_right(values, table3):
+    high, low = two_parts(values)
+    return jnp.dot(jnp.concatenate([high, low, high], 1), table3, preferred_element_type=F32)
+
+
+def plane_kernel(sticks_ref, base_ref, out_ref, rows_ref, *, points, bands, rows_py, planes):
+    px = pl.program_id(0)
+    xblock = out_ref.shape[3]
+    columns = sticks_ref.shape[4]
+    width = rows_py * columns
+    x_pos = jnp.concatenate([sticks_ref[0, 0, p, 14:15, :] for p in range(rows_py)], 1)
+    y_pos = jnp.concatenate([sticks_ref[0, 0, p, 15:16, :] for p in range(rows_py)], 1)
+    y_iota = lax.broadcasted_iota(jnp.int32, (points, width), 0)
+    picks = jnp.where(y_iota == y_pos.astype(jnp.int32), 1.0, 0.0).astype(BF16)
+    table = jnp.dot(base_ref[...], picks, preferred_element_type=F32).astype(BF16)
+    cos_high, cos_low, sin_high, sin_low = [
+        table[i * points : (i + 1) * points] for i in range(4)
+    ]
+    table_high = jnp.concatenate([cos_high, sin_high], 1)
+    table_low = jnp.concatenate([cos_low, sin_low], 1)
+    x_iota = lax.broadcasted_iota(jnp.int32, (xblock, width), 0) + px * xblock
+    mask = jnp.where(x_iota == x_pos.astype(jnp.int32), 1.0, 0.0).astype(F32)
+    half = bands * planes * xblock
+    for b in range(bands):
+        both = jnp.concatenate([sticks_ref[b, 0, p] for p in range(rows_py)], 1).astype(F32)
+        for z in range(planes):
+            real = (mask * both[z : z + 1]).astype(BF16)
+            imag = (mask * both[8 + z : 9 + z]).astype(BF16)
+            at = (b * planes + z) * xblock
+            rows_ref[at : at + xblock, :width] = real
+            rows_ref[at : at + xblock, width:] = -imag
+            rows_ref[half + at : half + at + xblock, :width] = imag
+            rows_ref[half + at : half + at + xblock, width:] = real
+    for part in range(2):
+        for b in range(bands):
+            at = (part * bands + b) * planes * xblock
+            rows = rows_ref[at : at + planes * xblock]
+            values = lax.dot_general(rows, table_high, LANE_DOT, preferred_element_type=F32)
+            values = values + lax.dot_general(rows, table_low, LANE_DOT, preferred_element_type=F32)
+            out_ref[part, b] = values.reshape(planes, xblock, points).astype(BF16)
+
+
+def density_kernel(
+    occ_ref, psi_ref, core_ref, xtab_ref, ytab_ref, ftab_ref, dl_ref, dr_ref,
+    send_ref, rho_ref, gx_ref, gy_ref, gsend_ref, *, bands, planes,
+):
+    points = core_ref.shape[1]
+    total = jnp.zeros((points, points), F32)
+    for b in range(bands):
+        real = psi_ref[0, b, 0]
+        imag = psi_ref[1, b, 0]
+        stacked = jnp.concatenate([real, real, imag, imag], 0)
+        psi = jnp.dot(xtab_ref[...], stacked, preferred_element_type=F32)
+        total = total + occ_ref[b] * (psi[:points] ** 2 + psi[points:] ** 2)
+    rho = total.T + core_ref[0]
+    rho_ref[0] = rho
+    grad_x = mul_right(rho, dr_ref[...])
+    grad_y = mul_left(dl_ref[...], rho)
+    gx_ref[0] = grad_x
+    gy_ref[0] = grad_y
+    rows_px, _, _, y_rows, _ = gsend_ref.shape
+    gsend_ref[:, 0, 0] = grad_x.reshape(rows_px, y_rows, points).astype(BF16)
+    gsend_ref[:, 1, 0] = grad_y.reshape(rows_px, y_rows, points).astype(BF16)
+    spectrum = mul_left(ytab_ref[...], mul_right(rho, ftab_ref[...]))
+    chunks = spectrum.reshape(send_ref.shape[0], ROW_PAD, send_ref.shape[3])
+    row = lax.broadcasted_iota(jnp.int32, chunks.shape, 1)
+    residual = chunks - chunks.astype(BF16).astype(F32)
+    send_ref[:, 0] = jnp.where(row == planes, residual, chunks).astype(BF16)
+
+
+def gather_rows(scratch, first, count):
+    parts = [
+        scratch[h, pl.ds(first, count, stride=ROW_PAD), :] for h in range(scratch.shape[0])
+    ]
+    return jnp.concatenate(parts, 1)
+
+
+def spectral_kernel(
+    place_ref, recv_ref, fwd_ref, inv_ref, der_ref, out_ref, in_scr, h_scr, g_scr, *, planes
+):
+    points = fwd_ref.shape[0]
+    sources = recv_ref.shape[0]
+    lanes = recv_ref.shape[3]
+    rows = sources * planes * ROW_PAD
+    halves = range(lanes // LANES)
+    arrived = recv_ref[...].astype(F32).reshape(rows, lanes)
+    for h in halves:
+        in_scr[h] = arrived[:, h * LANES : (h + 1) * LANES]
+    h_scr[...] = jnp.zeros_like(h_scr)
+    g_scr[...] = jnp.zeros_like(g_scr)
+    unit = (2.0 * math.pi / (points * SPACING)) ** 2
+    kz = lax.broadcasted_iota(jnp.int32, (points, lanes), 0)
+    kx = lax.broadcasted_iota(jnp.int32, (points, lanes), 1)
+    qz = jnp.minimum(kz, points - kz).astype(F32)
+    qx = jnp.minimum(kx, points - kx).astype(F32)
+    partial_square = qz * qz + qx * qx
+    for j in range(planes):
+        values = gather_rows(in_scr, j, points)
+        if j == 0:
+            values = values + gather_rows(in_scr, planes, points)
+        ky = place_ref[0] * planes + j
+        qy = jnp.minimum(ky, points - ky).astype(F32)
+        squared = unit * (partial_square + qy * qy)
+        factor = jnp.where(squared > 0, 4.0 * math.pi / jnp.where(squared > 0, squared, 1.0), 0.0)
+        scaled = factor * mul_left(fwd_ref[...], values)
+        hartree = mul_left(inv_ref[...], scaled)
+        grad_z = mul_left(der_ref[...], values)
+        for h in halves:
+            h_scr[h, pl.ds(j, points, stride=ROW_PAD), :] = hartree[:, h * LANES : (h + 1) * LANES]
+            g_scr[h, pl.ds(j, points, stride=ROW_PAD), :] = grad_z[:, h * LANES : (h + 1) * LANES]
+    shape = (sources, planes, ROW_PAD, LANES)
+    for h in halves:
+        at = slice(h * LANES, (h + 1) * LANES)
+        out_ref[:, 0, :, :, at] = h_scr[h].reshape(shape).astype(BF16)
+        out_ref[:, 1, :, :, at] = g_scr[h].reshape(shape).astype(BF16)
+
+
+def field_kernel(recv_ref, rho_ref, gx_ref, gy_ref, itab_ref, ytab_ref, send_ref):
+    points = rho_ref.shape[1]
+    rows = recv_ref.shape[0] * ROW_PAD
+    pieces = []
+    for f in range(2):
+        part = recv_ref[:, f, 0].astype(F32).reshape(rows, recv_ref.shape[4]).astype(BF16)
+        part = jnp.concatenate([part, part], 1)
+        part = jnp.dot(part, itab_ref[...], preferred_element_type=F32)
+        pieces.append(mul_left(ytab_ref[...], part))
+    hartree, grad_z = pieces
+    rho = rho_ref[0]
+    grad_x = gx_ref[0]
+    grad_y = gy_ref[0]
+    cube_root = jnp.exp(jnp.log(rho) * (1.0 / 3.0))
+    four_thirds = rho * cube_root
+    grad_square = grad_x * grad_x + grad_y * grad_y + grad_z * grad_z
+    reduced = grad_square / (REDUCED_SCALE * four_thirds * four_thirds)
+    denominator = 1.0 + PBE_MU * reduced / PBE_KAPPA
+    enhance = 1.0 + PBE_KAPPA - PBE_KAPPA / denominator
+    enhance_slope = PBE_MU / (denominator * denominator)
+    potential = hartree - SLATER_COEF * cube_root * (
+        4.0 / 3.0 * enhance - 8.0 / 3.0 * reduced * enhance_slope
+    )
+    rows_px, _, _, y_rows, _ = send_ref.shape
+    send_ref[:, 0, 0] = potential.reshape(rows_px, y_rows, points).astype(BF16)
+    send_ref[:, 1, 0] = grad_z.reshape(rows_px, y_rows, points).astype(BF16)
+
+
+def place_kernel(place_ref, early_ref, late_ref, *refs):
+    pot_ref, grad_ref = refs[-2:]
+    pot_ref[...] = late_ref[0, 0].astype(F32)
+    grad_ref[0] = early_ref[0, 0].astype(F32)
+    grad_ref[1] = early_ref[0, 1].astype(F32)
+    grad_ref[2] = late_ref[0, 1].astype(F32)
+
+
+def ring_gather(values, axis):
+    size = lax.axis_size(axis)
+    up = [(i, (i + 1) % size) for i in range(size)]
+    down = [(i, (i - 1) % size) for i in range(size)]
+    found = {0: values}
+    from_below = from_above = values
+    for step in range(1, size // 2 + 1):
+        if 2 * step == size:
+            cut = values.shape[0] // 2
+            low = lax.ppermute(from_below[:cut], axis, up)
+            high = lax.ppermute(from_above[cut:], axis, down)
+            found[step] = jnp.concatenate([low, high], 0)
+        else:
+            from_below = lax.ppermute(from_below, axis, up)
+            from_above = lax.ppermute(from_above, axis, down)
+            found[size - step] = from_below
+            found[step] = from_above
+    return found
+
+
+def slab_body(orbitals, occupations, stick_map, core_density):
+    _, columns, doubled = orbitals.shape
+    points = doubled // 2
+    bands = lax.axis_size("band")
+    rows_px = lax.axis_size("px")
+    rows_py = lax.axis_size("py")
+    band = lax.axis_index("band")
+    px = lax.axis_index("px")
+    py = lax.axis_index("py")
+    devices = bands * rows_px * rows_py
+    planes = points // devices
+    xblock = y_rows = points // rows_px
+    zblock = points // rows_py
+    zshare = zblock // bands
+    cosine, sine = wave_tables(points)
+    grid = np.arange(devices)
+    starts = (
+        grid % rows_py * zblock
+        + grid // (rows_px * rows_py) * zshare
+        + grid // rows_py % rows_px * planes
+    )
+    z_order = starts[:, None] + np.arange(planes)
+
+    picked = np.zeros((devices, 2, 8, doubled))
+    picked[:, 0, :planes] = np.concatenate([cosine[z_order], -sine[z_order]], -1)
+    picked[:, 1, :planes] = np.concatenate([sine[z_order], cosine[z_order]], -1)
+    high, low = split_table(picked.reshape(devices * 16, doubled))
+    source = orbitals.reshape(columns, doubled)
+    waves = lax.dot_general(high, source, LANE_DOT, preferred_element_type=F32)
+    waves = waves + lax.dot_general(low, source, LANE_DOT, preferred_element_type=F32)
+    waves = waves.reshape(devices, 16, columns)
+    own = lax.dynamic_slice_in_dim(stick_map, py * columns, columns, 1).astype(F32)
+    occ = jnp.broadcast_to(occupations.reshape(1, 1), (1, columns))
+    occ_high = occ.astype(BF16).astype(F32)
+    occ_mid = (occ - occ_high).astype(BF16).astype(F32)
+    occ_low = occ - occ_high - occ_mid
+    lane = jnp.arange(columns)[None, :]
+    extra = jnp.concatenate([occ_high, jnp.where(lane < columns // 2, occ_mid, occ_low)], 0)
+    zeros = jnp.zeros((6, columns), F32)
+    extra = jnp.concatenate([zeros, extra, zeros, own], 0)
+    row = lax.broadcasted_iota(jnp.int32, waves.shape, 1)
+    waves = jnp.where(row % 8 >= planes, extra[None], waves).astype(BF16)
+    sticks = lax.all_to_all(waves, AXES, split_axis=0, concat_axis=0, tiled=True)
+    sticks = sticks.reshape(bands, rows_px, rows_py, 16, columns)
+    core = lax.dynamic_slice_in_dim(core_density, band * zshare, zshare, 0)
+    core = lax.all_to_all(core, "px", split_axis=0, concat_axis=1, tiled=True)
+    occ_all = sticks[:, 0, 0, 6, 0].astype(F32) + (
+        sticks[:, 0, 0, 7, 0].astype(F32) + sticks[:, 0, 0, 7, columns - 1].astype(F32)
+    )
+
+    cos_high, cos_low = split_table(cosine)
+    sin_high, sin_low = split_table(sine)
+    base = np.concatenate([cos_high, cos_low, sin_high, sin_low], 0)
+    psi_y = pl.pallas_call(
+        lambda *refs: plane_kernel(
+            *refs, points=points, bands=bands, rows_py=rows_py, planes=planes
+        ),
+        grid=(rows_px,),
+        in_specs=[
+            pl.BlockSpec((bands, 1, rows_py, 16, columns), lambda i: (0, i, 0, 0, 0)),
+            pl.BlockSpec(base.shape, lambda i: (0, 0)),
+        ],
+        out_specs=pl.BlockSpec((2, bands, planes, xblock, points), lambda i: (0, 0, 0, i, 0)),
+        out_shape=jax.ShapeDtypeStruct((2, bands, planes, points, points), BF16),
+        scratch_shapes=[pltpu.VMEM((2 * bands * planes * xblock, 2 * rows_py * columns), BF16)],
+        name="planes",
+    )(sticks, base)
+
+    basis = real_basis(points)
+    slope = derivative(points)
+    lanes = -(-points // LANES) * LANES
+    basis_lanes = np.zeros((points, lanes))
+    basis_lanes[:, :points] = basis.T
+    padded = np.zeros((devices, ROW_PAD, points))
+    padded[:, :planes] = basis.reshape(devices, planes, points)
+    inverse_pad = padded.reshape(devices * ROW_PAD, points).T.copy()
+    padded[:, planes] = padded[:, 0]
+    forward_pad = padded.reshape(devices * ROW_PAD, points)
+    x_table = np.concatenate(
+        [
+            np.concatenate([cos_high, cos_low, -sin_high, -sin_low], 1),
+            np.concatenate([sin_high, sin_low, cos_high, cos_low], 1),
+        ],
+        0,
+    )
+    tables = [
+        x_table, left3(forward_pad), right3(basis_lanes), left3(slope), right3(slope.T),
+    ]
+    whole = lambda t: pl.BlockSpec(t.shape, lambda i: (0,) * t.ndim)
+    plane_spec = pl.BlockSpec((1, points, points), lambda i: (i, 0, 0))
+    plane_shape = jax.ShapeDtypeStruct((planes, points, points), F32)
+    pair_spec = pl.BlockSpec((rows_px, 2, 1, y_rows, points), lambda i: (0, 0, i, 0, 0))
+    pair_shape = jax.ShapeDtypeStruct((rows_px, 2, planes, y_rows, points), BF16)
+    sent, rho, grad_x, grad_y, early = pl.pallas_call(
+        lambda *refs: density_kernel(*refs, bands=bands, planes=planes),
+        grid=(planes,),
+        in_specs=[
+            pl.BlockSpec(memory_space=pltpu.SMEM),
+            pl.BlockSpec((2, bands, 1, points, points), lambda i: (0, 0, i, 0, 0)),
+            plane_spec,
+        ] + [whole(t) for t in tables],
+        out_specs=[
+            pl.BlockSpec((devices, 1, ROW_PAD, lanes), lambda i: (0, i, 0, 0)),
+            plane_spec, plane_spec, plane_spec, pair_spec,
+        ],
+        out_shape=[
+            jax.ShapeDtypeStruct((devices, planes, ROW_PAD, lanes), BF16),
+            plane_shape, plane_shape, plane_shape, pair_shape,
+        ],
+        name="density",
+    )(occ_all, psi_y, core, *tables)
+
+    spread = lax.all_to_all(sent, AXES, split_axis=0, concat_axis=0, tiled=True)
+    early = lax.all_to_all(early, "px", split_axis=0, concat_axis=0, tiled=True)
+    early = ring_gather(early, "band")
+
+    place = ((band * rows_px + px) * rows_py + py).reshape(1)
+    order = z_order.reshape(-1)
+    z_tables = [
+        left3(basis[:, order]), left3(basis.T[order]), left3(slope[order][:, order]),
+    ]
+    rows = points * ROW_PAD
+    spread = pl.pallas_call(
+        lambda *refs: spectral_kernel(*refs, planes=planes),
+        in_specs=[pl.BlockSpec(memory_space=pltpu.SMEM)]
+        + [pl.BlockSpec(memory_space=pltpu.VMEM)] * 4,
+        out_specs=pl.BlockSpec(memory_space=pltpu.VMEM),
+        out_shape=jax.ShapeDtypeStruct((devices, 2, planes, ROW_PAD, lanes), BF16),
+        scratch_shapes=[pltpu.VMEM((lanes // LANES, rows, LANES), F32)] * 3,
+        name="spectral",
+    )(place, spread, *z_tables)
+    spread = lax.all_to_all(spread, AXES, split_axis=0, concat_axis=0, tiled=True)
+
+    basis_high, basis_low = split_table(basis_lanes.T)
+    back_tables = [np.concatenate([basis_high, basis_low], 0), left3(inverse_pad)]
+    late = pl.pallas_call(
+        field_kernel,
+        grid=(planes,),
+        in_specs=[
+            pl.BlockSpec((devices, 2, 1, ROW_PAD, lanes), lambda i: (0, 0, i, 0, 0)),
+            plane_spec, plane_spec, plane_spec,
+        ] + [whole(t) for t in back_tables],
+        out_specs=pair_spec,
+        out_shape=pair_shape,
+        name="fields",
+    )(spread, rho, grad_x, grad_y, *back_tables)
+    late = lax.all_to_all(late, "px", split_axis=0, concat_axis=0, tiled=True)
+    late = ring_gather(late, "band")
+
+    out_shape = [
+        jax.ShapeDtypeStruct((zblock, y_rows, points), F32),
+        jax.ShapeDtypeStruct((3, zblock, y_rows, points), F32),
+    ]
+    results = []
+    for shift in range(bands):
+        index = ((band + shift) % bands).reshape(1)
+        piece = pl.BlockSpec((1, 2, planes, y_rows, points), lambda i, s: (i, 0, 0, 0, 0))
+        results = pl.pallas_call(
+            place_kernel,
+            grid_spec=pltpu.PrefetchScalarGridSpec(
+                num_scalar_prefetch=1,
+                grid=(rows_px,),
+                in_specs=[piece, piece] + [pl.BlockSpec(memory_space=pl.ANY)] * len(results),
+                out_specs=[
+                    pl.BlockSpec(
+                        (planes, y_rows, points), lambda i, s: (s[0] * rows_px + i, 0, 0)
+                    ),
+                    pl.BlockSpec(
+                        (3, planes, y_rows, points), lambda i, s: (0, s[0] * rows_px + i, 0, 0)
+                    ),
+                ],
+            ),
+            out_shape=out_shape,
+            input_output_aliases={3: 0, 4: 1} if results else {},
+            name="place",
+        )(index, early[shift], late[shift], *results)
+    return tuple(results)
+
+
+def body(orbitals, occupations, stick_map, core_density):
+    points = orbitals.shape[2] // 2
+    devices = lax.axis_size("band") * lax.axis_size("px") * lax.axis_size("py")
+    planes = points // devices
+    whole_planes = points % (2 * devices) == 0 and planes < 7 and points <= 256
+    if whole_planes and orbitals.shape[0] == 1 and orbitals.shape[1] % 128 == 0:
+        return slab_body(orbitals, occupations, stick_map, core_density)
+    return pencil_body(orbitals, occupations, stick_map, core_density)
+
+
 def solution(mesh):
     return jax.shard_map(
         body,

time: 1170 us -> 316 us (0.27)
  waiting for transfers between devices: 584 us -> 122 us
  local copies, waits for them, and re-layouts: 291 us -> 8.63 us
  matrix products: 103 us -> 2.52 us
  other arithmetic: 98.1 us -> 7.69 us
  starting transfers between devices: 22.4 us -> 78.5 us
  Pallas kernels: 0 us -> 52.3 us
  between operations: 15.5 us -> 1.51 us
    all_gather x1 -> x0, waiting for transfers between devices: 320 us -> none  [body(): lax.all_gather(exchange_part(rho_local, fields), 'band', axis=1, tiled=True)]
    reshape x15 -> x0, local copies, waits for them, and re-layouts: 162 us -> none  [the longest x2 30.3 us: transform(): section_data = section_data.reshape(points, 2, zshare, 2, y_rows)]
    all_to_all x5, waiting for transfers between devices: 179 us -> 52.1 us  [the longest x1 20.6 us: slab_body(): spread = lax.all_to_all(sent, AXES, split_axis=0, concat_axis=0, tiled=True)]
    dot_general x9 -> x2, matrix products: 103 us -> 2.52 us  [the longest x1 1.26 us: slab_body(): lax.dot_general(low, source, LANE_DOT, preferred_element_type=F32)]
    reduce_scatter x1 -> x0, waiting for transfers between devices: 84.4 us -> none  [body(): lax.psum_scatter(density, 'band', scatter_dimension=0, tiled=True)]
    unnamed x2 -> x0, other arithmetic: 79.7 us -> none
    ppermute x0 -> x8, waiting for transfers between devices: none -> 70.3 us  [the longest x2 33.9 us: ring_gather(): from_below = lax.ppermute(from_below, axis, up)]
    ppermute x0 -> x8, starting transfers between devices: none -> 58 us  [the longest x2 46.9 us: ring_gather(): low = lax.ppermute(from_below[:cut], axis, up)]
  transfers between devices with their start and end apart: 7 -> 13, of which waited for: 7 -> 12; matrix products, arithmetic and copies ran while one was open for 1% -> 3% of each run, Pallas kernels for 0% -> 8%
where the time goes in v1:
time: 316 us; the launch traced here: 315 us
  waiting for transfers between devices  122 us (39%)
  starting transfers between devices  78.5 us (25%)
  Pallas kernels  52.3 us (17%)
  blocking collectives  41.1 us (13%)
  local copies, waits for them, and re-layouts  8.63 us (3%)
  other arithmetic  7.69 us (2%)
    ppermute x2, starting transfers between devices, ring_gather(): low = lax.ppermute(from_below[:cut], axis, up)  46.9 us
    all_to_all x1, blocking collectives, slab_body(): lax.all_to_all(spread, AXES, split_axis=0, concat_axis=0, tiled=True)  41.1 us
    ppermute x2, waiting for transfers between devices, ring_gather(): from_below = lax.ppermute(from_below, axis, up)  33.9 us
    ppermute x2, waiting for transfers between devices, ring_gather(): high = lax.ppermute(from_above[cut:], axis, down)  22 us
    all_to_all x1, waiting for transfers between devices, slab_body(): spread = lax.all_to_all(sent, AXES, split_axis=0, concat_axis=0, tiled=True)  20.6 us
    pallas_call x4, Pallas kernels, slab_body(): pl.pallas_call(place_kernel, grid_spec=pltpu.PrefetchScalarGridSpec(num_s...  17.1 us
    ppermute x2, waiting for transfers between devices, ring_gather(): low = lax.ppermute(from_below[:cut], axis, up)  13.9 us
    pallas_call x1, Pallas kernels, slab_body(): pl.pallas_call(lambda *refs: density_kernel(*refs, bands=bands, planes=pl...  12.8 us
  transfers between devices with their start and end apart: 13, of which 12 were waited for; matrix products, arithmetic and copies ran while one was open for 3% of the time, Pallas kernels for 8%

profile of v1, /device:TPU:0, one launch (start us, length us, event | category | flops | bytes accessed | tf_op | source)
XLA Modules:
  0.0 314.6 jit_solution(3802266433305664379)
XLA Ops:
  5.4 7.3 %all-to-all-start = ((bf16[32,16,128]{2,1,0:T(8,128)(2,1)}), bf16[32,16,128]{2,1,0:T(8,128)(2,1)S(1)}, u32[]{:S(2)}, u32[]{:S(2)}) async-start(bf16[32,16,128]{2,1,0:T(8,128)(2,1)} %select_convert_fusion), calls=%async_computation | async-start | bytes 262144 | tf_op jit(solution)/shard_map/all_to_all | solution.py:447
  15.2 6.2 %all-to-all-done = bf16[32,16,128]{2,1,0:T(8,128)(2,1)S(1)} async-done(((bf16[32,16,128]{2,1,0:T(8,128)(2,1)}), bf16[32,16,128]{2,1,0:T(8,128)(2,1)S(1)}, u32[]{:S(2)}, u32[]{:S(2)}) %all-to-all-start) | async-done | bytes 131104 | tf_op jit(solution)/shard_map/all_to_all | solution.py:447
  21.4 3.5 %all-to-all-start.1 = ((f32[24,48,192]{2,1,0:T(8,128)}), f32[24,48,192]{2,1,0:T(8,128)S(1)}, u32[]{:S(2)}, u32[]{:S(2)}) async-start(f32[24,48,192]{2,1,0:T(8,128)} %constant_dynamic-slice_fusion), calls=%async_computation.1 | async-start | bytes 2359296 | tf_op jit(solution)/shard_map/all_to_all | solution.py:450
  24.9 8.7 %planes.1.refs_1_ = bf16[2,4,6,192,192]{4,3,2,1,0:T(8,128)(2,1)} custom-call(bf16[4,4,2,16,128]{4,3,2,1,0:T(8,128)(2,1)} %bitcast.24, bf16[768,192]{1,0:T(8,128)(2,1)} %constant.99.clone.refs_1_), custom_call_target="tpu_custom_call" | custom-call | tf_op jit(solution)/shard_map/planes/pallas_call | solution.py:458
  35.1 5.6 %all-to-all-done.1 = f32[24,48,192]{2,1,0:T(8,128)S(1)} async-done(((f32[24,48,192]{2,1,0:T(8,128)}), f32[24,48,192]{2,1,0:T(8,128)S(1)}, u32[]{:S(2)}, u32[]{:S(2)}) %all-to-all-start.1) | async-done | bytes 884768 | tf_op jit(solution)/shard_map/all_to_all | solution.py:450
  41.8 12.8 %density.1 = (bf16[32,6,8,256]{3,2,1,0:T(8,128)(2,1)}, f32[6,192,192]{2,1,0:T(8,128)}, f32[6,192,192]{2,1,0:T(8,128)}, f32[6,192,192]{2,1,0:T(8,128)}, bf16[4,2,6,48,192]{4,3,2,1,0:T(8,128)(2,1)}) custom-call(f32[4]{0:T(128)} %fusion.5.refs_0_, bf16[2,4,6,192,192]{4,3,2,1,0:T(8,128)(2,1)} %planes.1.refs_1_, f32[6,192,192]{2,1,0:T(8,128)} %bitcast.23, ...), custom_call_target="tpu_custom_call" | custom-call | tf_op jit(solution)/shard_map/density/pallas_call | solution.py:498
  57.3 20.6 %all-to-all-done.3.refs_1_ = bf16[32,6,8,256]{3,2,1,0:T(8,128)(2,1)S(1)} async-done(((bf16[32,6,8,256]{3,2,1,0:T(8,128)(2,1)}), bf16[32,6,8,256]{3,2,1,0:T(8,128)(2,1)S(1)}, u32[]{:S(2)}, u32[]{:S(2)}) %all-to-all-start.3) | async-done | bytes 786464 | tf_op jit(solution)/shard_map/all_to_all | solution.py:517
  78.7 5.7 %spectral.1 = bf16[32,2,6,8,256]{4,3,2,1,0:T(8,128)(2,1)} custom-call(s32[1]{0:T(128)} %bitcast.10.refs_0_, bf16[32,6,8,256]{3,2,1,0:T(8,128)(2,1)} %copy-done.3, bf16[192,576]{1,0:T(8,128)(2,1)} %constant.105.clone.refs_2_, bf16[192,576]{1,0:T(8,128)(2,1)} %constant.106.clone.refs_3_, bf16[192,576]{1,0:T(8,128)(2,1)} %constant.107.clone.refs_4_), custom_call_target="tpu_custom_call" | custom-call | tf_op jit(solution)/shard_map/spectral/pallas_call | solution.py:527
  84.4 41.1 %all_to_all.43.recv_ref = bf16[32,2,6,8,256]{4,3,2,1,0:T(8,128)(2,1)} all-to-all(bf16[32,2,6,8,256]{4,3,2,1,0:T(8,128)(2,1)} %spectral.1), channel_id=1, replica_groups=mesh['band'=4,'px'=4,'py'=2] {'band','px','py'}, dimensions={0} | all-to-all | bytes 3145728 | tf_op jit(solution)/shard_map/all_to_all | solution.py:536
  129.0 8.1 %fields.1 = bf16[4,2,6,48,192]{4,3,2,1,0:T(8,128)(2,1)} custom-call(bf16[32,2,6,8,256]{4,3,2,1,0:T(8,128)(2,1)} %all_to_all.43.recv_ref, f32[6,192,192]{2,1,0:T(8,128)} %get-tuple-element.15.rho_ref, f32[6,192,192]{2,1,0:T(8,128)} %get-tuple-element.16.gx_ref, f32[6,192,192]{2,1,0:T(8,128)} %get-tuple-element.17.gy_ref, ...), custom_call_target="tpu_custom_call" | custom-call | tf_op jit(solution)/shard_map/fields/pallas_call | solution.py:540
  137.1 7.7 %all-to-all-done.2.early_ref = bf16[4,2,6,48,192]{4,3,2,1,0:T(8,128)(2,1)S(1)} async-done(((bf16[4,2,6,48,192]{4,3,2,1,0:T(8,128)(2,1)}), bf16[4,2,6,48,192]{4,3,2,1,0:T(8,128)(2,1)S(1)}, u32[]{:S(2)}, u32[]{:S(2)}) %all-to-all-start.2) | async-done | bytes 884768 | tf_op jit(solution)/shard_map/all_to_all | solution.py:518
  144.9 3.5 %all-to-all-start.5 = ((bf16[4,2,6,48,192]{4,3,2,1,0:T(8,128)(2,1)}), bf16[4,2,6,48,192]{4,3,2,1,0:T(8,128)(2,1)S(1)}, u32[]{:S(2)}, u32[]{:S(2)}) async-start(bf16[4,2,6,48,192]{4,3,2,1,0:T(8,128)(2,1)} %fields.1), calls=%async_computation.5 | async-start | bytes 2359296 | tf_op jit(solution)/shard_map/all_to_all | solution.py:551
  152.3 11.9 %all-to-all-done.5.late_ref = bf16[4,2,6,48,192]{4,3,2,1,0:T(8,128)(2,1)S(1)} async-done(((bf16[4,2,6,48,192]{4,3,2,1,0:T(8,128)(2,1)}), bf16[4,2,6,48,192]{4,3,2,1,0:T(8,128)(2,1)S(1)}, u32[]{:S(2)}, u32[]{:S(2)}) %all-to-all-start.5) | async-done | bytes 884768 | tf_op jit(solution)/shard_map/all_to_all | solution.py:551
  168.0 11.2 %collective-permute-done.early_ref = bf16[4,2,6,48,192]{4,3,2,1,0:T(8,128)(2,1)} collective-permute-done((bf16[4,2,6,48,192]{4,3,2,1,0:T(8,128)(2,1)S(1)}, bf16[4,2,6,48,192]{4,3,2,1,0:T(8,128)(2,1)}, u32[]{:S(2)}, u32[]{:S(2)}) %collective-permute-start) | collective-permute-done | bytes 884768 | tf_op jit(solution)/shard_map/ppermute | solution.py:398
  180.3 23.4 %collective-permute-start.2 = (bf16[2,2,6,48,192]{4,3,2,1,0:T(8,128)(2,1)S(1)}, bf16[2,2,6,48,192]{4,3,2,1,0:T(8,128)(2,1)}, u32[]{:S(2)}, u32[]{:S(2)}) collective-permute-start(bf16[2,2,6,48,192]{4,3,2,1,0:T(8,128)(2,1)S(1)} %slice.31), channel_id=1, source_target_pairs={{0,8},{8,16},{16,24},{24,0},{1,9},{9,17},{17,25},{25,1},{2,10},{10... | collective-permute-start | bytes 1327112 | tf_op jit(solution)/shard_map/ppermute | solution.py:394
  207.1 22.6 %collective-permute-done.1.late_ref = bf16[4,2,6,48,192]{4,3,2,1,0:T(8,128)(2,1)S(1)} collective-permute-done((bf16[4,2,6,48,192]{4,3,2,1,0:T(8,128)(2,1)S(1)}, bf16[4,2,6,48,192]{4,3,2,1,0:T(8,128)(2,1)S(1)}, u32[]{:S(2)}, u32[]{:S(2)}) %collective-permute-start.1) | collective-permute-done | bytes 884768 | tf_op jit(solution)/shard_map/ppermute | solution.py:398
  229.8 23.5 %collective-permute-start.5 = (bf16[2,2,6,48,192]{4,3,2,1,0:T(8,128)(2,1)S(1)}, bf16[2,2,6,48,192]{4,3,2,1,0:T(8,128)(2,1)}, u32[]{:S(2)}, u32[]{:S(2)}) collective-permute-start(bf16[2,2,6,48,192]{4,3,2,1,0:T(8,128)(2,1)S(1)} %slice.33), channel_id=1, source_target_pairs={{0,8},{8,16},{16,24},{24,0},{1,9},{9,17},{17,25},{25,1},{2,10},{10... | collective-permute-start | bytes 1327112 | tf_op jit(solution)/shard_map/ppermute | solution.py:394
  256.9 10.9 %collective-permute-done.2 = bf16[2,2,6,48,192]{4,3,2,1,0:T(8,128)(2,1)} collective-permute-done((bf16[2,2,6,48,192]{4,3,2,1,0:T(8,128)(2,1)S(1)}, bf16[2,2,6,48,192]{4,3,2,1,0:T(8,128)(2,1)}, u32[]{:S(2)}, u32[]{:S(2)}) %collective-permute-start.2) | collective-permute-done | bytes 442400 | tf_op jit(solution)/shard_map/ppermute | solution.py:394
  267.8 11.4 %collective-permute-done.4 = bf16[2,2,6,48,192]{4,3,2,1,0:T(8,128)(2,1)} collective-permute-done((bf16[2,2,6,48,192]{4,3,2,1,0:T(8,128)(2,1)}, bf16[2,2,6,48,192]{4,3,2,1,0:T(8,128)(2,1)}, u32[]{:S(2)}, u32[]{:S(2)}) %collective-permute-start.4) | collective-permute-done | bytes 442400 | tf_op jit(solution)/shard_map/ppermute | solution.py:395
  281.6 4.3 %place.4 = (f32[96,48,192]{2,1,0:T(8,128)}, f32[3,96,48,192]{3,2,1,0:T(8,128)}) custom-call(s32[1]{0:T(128)} %bitcast.13.place_ref, bf16[4,2,6,48,192]{4,3,2,1,0:T(8,128)(2,1)} %copy-done.1, bf16[4,2,6,48,192]{4,3,2,1,0:T(8,128)(2,1)} %copy-done.2), custom_call_target="tpu_custom_call" | custom-call | tf_op jit(solution)/shard_map/place/pallas_call | solution.py:562
  285.9 4.3 %place.5 = (f32[96,48,192]{2,1,0:T(8,128)}, f32[3,96,48,192]{3,2,1,0:T(8,128)}) custom-call(s32[1]{0:T(128)} %bitcast.12.place_ref, bf16[4,2,6,48,192]{4,3,2,1,0:T(8,128)(2,1)} %collective-permute-done.3.early_ref, bf16[4,2,6,48,192]{4,3,2,1,0:T(8,128)(2,1)} %copy-done.5, ...), custom_call_target="tpu_custom_call", output_to_operand_aliasing={{0}: (3, {}), {1}: (4, {})} | custom-call | tf_op jit(solution)/shard_map/place/pallas_call | solution.py:562
  293.1 10.7 %collective-permute-done.7 = bf16[2,2,6,48,192]{4,3,2,1,0:T(8,128)(2,1)S(1)} collective-permute-done((bf16[2,2,6,48,192]{4,3,2,1,0:T(8,128)(2,1)S(1)}, bf16[2,2,6,48,192]{4,3,2,1,0:T(8,128)(2,1)S(1)}, u32[]{:S(2)}, u32[]{:S(2)}) %collective-permute-start.7) | collective-permute-done | bytes 442400 | tf_op jit(solution)/shard_map/ppermute | solution.py:395
  306.0 4.3 %place.6 = (f32[96,48,192]{2,1,0:T(8,128)}, f32[3,96,48,192]{3,2,1,0:T(8,128)}) custom-call(s32[1]{0:T(128)} %bitcast.11.place_ref, bf16[4,2,6,48,192]{4,3,2,1,0:T(8,128)(2,1)} %pad_maximum_fusion.early_ref, bf16[4,2,6,48,192]{4,3,2,1,0:T(8,128)(2,1)} %pad_maximum_fusion.1.late_ref, ...), custom_call_target="tpu_custom_call", output_to_operand_aliasing={{0}: (3, {}), {1}: (4, {})} | custom-call | tf_op jit(solution)/shard_map/place/pallas_call | solution.py:562
  310.3 4.3 %place.7 = (f32[96,48,192]{2,1,0:T(8,128)}, f32[3,96,48,192]{3,2,1,0:T(8,128)}) custom-call(s32[1]{0:T(128)} %bitcast.place_ref, bf16[4,2,6,48,192]{4,3,2,1,0:T(8,128)(2,1)} %collective-permute-done.early_ref, bf16[4,2,6,48,192]{4,3,2,1,0:T(8,128)(2,1)} %copy-done.4, ...), custom_call_target="tpu_custom_call", output_to_operand_aliasing={{0}: (3, {}), {1}: (4, {})} | custom-call | tf_op jit(solution)/shard_map/place/pallas_call | solution.py:562
  (44 shorter events, 39.5 us)
Async XLA Ops:
  0.6 1.4 copy-start
  5.4 15.9 %all-to-all-start = ((bf16[32,16,128]{2,1,0:T(8,128)(2,1)}), bf16[32,16,128]{2,1,0:T(8,128)(2,1)S(1)}, u32[]{:S(2)}, u32[]{:S(2)}) async-start(bf16[32,16,128]{2,1,0:T(8,128)(2,1)} %select_convert_fusion), calls=%async_computation | async-start | bytes 262144 | tf_op jit(solution)/shard_map/all_to_all | solution.py:447
  21.4 3.5 %copy-start.6 = (bf16[32,16,128]{2,1,0:T(8,128)(2,1)}, bf16[32,16,128]{2,1,0:T(8,128)(2,1)S(1)}, u32[]{:S(2)}) copy-start(bf16[32,16,128]{2,1,0:T(8,128)(2,1)S(1)} %all-to-all-done) | copy-start | bytes 393220
  21.4 19.3 %all-to-all-start.1 = ((f32[24,48,192]{2,1,0:T(8,128)}), f32[24,48,192]{2,1,0:T(8,128)S(1)}, u32[]{:S(2)}, u32[]{:S(2)}) async-start(f32[24,48,192]{2,1,0:T(8,128)} %constant_dynamic-slice_fusion), calls=%async_computation.1 | async-start | bytes 2359296 | tf_op jit(solution)/shard_map/all_to_all | solution.py:450
  54.6 23.2 %all-to-all-start.3 = ((bf16[32,6,8,256]{3,2,1,0:T(8,128)(2,1)}), bf16[32,6,8,256]{3,2,1,0:T(8,128)(2,1)S(1)}, u32[]{:S(2)}, u32[]{:S(2)}) async-start(bf16[32,6,8,256]{3,2,1,0:T(8,128)(2,1)} %get-tuple-element.14), calls=%async_computation.3 | async-start | bytes 1572864 | tf_op jit(solution)/shard_map/all_to_all | solution.py:517
  77.8 0.9 copy-start.3
  125.5 19.3 %all-to-all-start.2 = ((bf16[4,2,6,48,192]{4,3,2,1,0:T(8,128)(2,1)}), bf16[4,2,6,48,192]{4,3,2,1,0:T(8,128)(2,1)S(1)}, u32[]{:S(2)}, u32[]{:S(2)}) async-start(bf16[4,2,6,48,192]{4,3,2,1,0:T(8,128)(2,1)} %get-tuple-element.13), calls=%async_computation.2 | async-start | bytes 2359296 | tf_op jit(solution)/shard_map/all_to_all | solution.py:518
  144.8 4.2 %copy-start.1 = (bf16[4,2,6,48,192]{4,3,2,1,0:T(8,128)(2,1)}, bf16[4,2,6,48,192]{4,3,2,1,0:T(8,128)(2,1)S(1)}, u32[]{:S(2)}) copy-start(bf16[4,2,6,48,192]{4,3,2,1,0:T(8,128)(2,1)S(1)} %all-to-all-done.2.early_ref) | copy-start | bytes 2654212
  144.9 19.3 %all-to-all-start.5 = ((bf16[4,2,6,48,192]{4,3,2,1,0:T(8,128)(2,1)}), bf16[4,2,6,48,192]{4,3,2,1,0:T(8,128)(2,1)S(1)}, u32[]{:S(2)}, u32[]{:S(2)}) async-start(bf16[4,2,6,48,192]{4,3,2,1,0:T(8,128)(2,1)} %fields.1), calls=%async_computation.5 | async-start | bytes 2359296 | tf_op jit(solution)/shard_map/all_to_all | solution.py:551
  148.4 30.8 %collective-permute-start = (bf16[4,2,6,48,192]{4,3,2,1,0:T(8,128)(2,1)S(1)}, bf16[4,2,6,48,192]{4,3,2,1,0:T(8,128)(2,1)}, u32[]{:S(2)}, u32[]{:S(2)}) collective-permute-start(bf16[4,2,6,48,192]{4,3,2,1,0:T(8,128)(2,1)S(1)} %all-to-all-done.2.early_ref), channel_id=1, source_target_pairs={{0,8},{8,16},{16,24},{24,0},{1,9},{9,17},{17,25},{25,1},{2,10},{10... | collective-permute-start | bytes 2654216 | tf_op jit(solution)/shard_map/ppermute | solution.py:398
  149.1 54.7 %collective-permute-start.3 = (bf16[4,2,6,48,192]{4,3,2,1,0:T(8,128)(2,1)S(1)}, bf16[4,2,6,48,192]{4,3,2,1,0:T(8,128)(2,1)}, u32[]{:S(2)}, u32[]{:S(2)}) collective-permute-start(bf16[4,2,6,48,192]{4,3,2,1,0:T(8,128)(2,1)S(1)} %all-to-all-done.2.early_ref), channel_id=1, source_target_pairs={{0,24},{8,0},{16,8},{24,16},{1,25},{9,1},{17,9},{25,17},{2,26},{10... | collective-permute-start | bytes 2654216 | tf_op jit(solution)/shard_map/ppermute | solution.py:399
  164.2 41.5 %copy-start.2 = (bf16[4,2,6,48,192]{4,3,2,1,0:T(8,128)(2,1)}, bf16[4,2,6,48,192]{4,3,2,1,0:T(8,128)(2,1)S(1)}, u32[]{:S(2)}) copy-start(bf16[4,2,6,48,192]{4,3,2,1,0:T(8,128)(2,1)S(1)} %all-to-all-done.5.late_ref) | copy-start | bytes 2654212
  164.2 65.5 %collective-permute-start.1 = (bf16[4,2,6,48,192]{4,3,2,1,0:T(8,128)(2,1)S(1)}, bf16[4,2,6,48,192]{4,3,2,1,0:T(8,128)(2,1)S(1)}, u32[]{:S(2)}, u32[]{:S(2)}) collective-permute-start(bf16[4,2,6,48,192]{4,3,2,1,0:T(8,128)(2,1)S(1)} %all-to-all-done.5.late_ref), channel_id=1, source_target_pairs={{0,8},{8,16},{16,24},{24,0},{1,9},{9,17},{17,25},{25,1},{2,10},{10... | collective-permute-start | bytes 2654216 | tf_op jit(solution)/shard_map/ppermute | solution.py:398
  164.8 88.9 %collective-permute-start.6 = (bf16[4,2,6,48,192]{4,3,2,1,0:T(8,128)(2,1)S(1)}, bf16[4,2,6,48,192]{4,3,2,1,0:T(8,128)(2,1)S(1)}, u32[]{:S(2)}, u32[]{:S(2)}) collective-permute-start(bf16[4,2,6,48,192]{4,3,2,1,0:T(8,128)(2,1)S(1)} %all-to-all-done.5.late_ref), channel_id=1, source_target_pairs={{0,24},{8,0},{16,8},{24,16},{1,25},{9,1},{17,9},{25,17},{2,26},{10... | collective-permute-start | bytes 2654216 | tf_op jit(solution)/shard_map/ppermute | solution.py:399
  180.3 87.5 %collective-permute-start.2 = (bf16[2,2,6,48,192]{4,3,2,1,0:T(8,128)(2,1)S(1)}, bf16[2,2,6,48,192]{4,3,2,1,0:T(8,128)(2,1)}, u32[]{:S(2)}, u32[]{:S(2)}) collective-permute-start(bf16[2,2,6,48,192]{4,3,2,1,0:T(8,128)(2,1)S(1)} %slice.31), channel_id=1, source_target_pairs={{0,8},{8,16},{16,24},{24,0},{1,9},{9,17},{17,25},{25,1},{2,10},{10... | collective-permute-start | bytes 1327112 | tf_op jit(solution)/shard_map/ppermute | solution.py:394
  205.7 73.5 %collective-permute-start.4 = (bf16[2,2,6,48,192]{4,3,2,1,0:T(8,128)(2,1)}, bf16[2,2,6,48,192]{4,3,2,1,0:T(8,128)(2,1)}, u32[]{:S(2)}, u32[]{:S(2)}) collective-permute-start(bf16[2,2,6,48,192]{4,3,2,1,0:T(8,128)(2,1)} %slice.32), channel_id=1, source_target_pairs={{0,24},{8,0},{16,8},{24,16},{1,25},{9,1},{17,9},{25,17},{2,26},{10... | collective-permute-start | bytes 1327112 | tf_op jit(solution)/shard_map/ppermute | solution.py:395
  229.7 25.2 %copy-start.4 = (bf16[4,2,6,48,192]{4,3,2,1,0:T(8,128)(2,1)}, bf16[4,2,6,48,192]{4,3,2,1,0:T(8,128)(2,1)S(1)}, u32[]{:S(2)}) copy-start(bf16[4,2,6,48,192]{4,3,2,1,0:T(8,128)(2,1)S(1)} %collective-permute-done.1.late_ref) | copy-start | bytes 2654212
  229.8 63.3 %collective-permute-start.5 = (bf16[2,2,6,48,192]{4,3,2,1,0:T(8,128)(2,1)S(1)}, bf16[2,2,6,48,192]{4,3,2,1,0:T(8,128)(2,1)}, u32[]{:S(2)}, u32[]{:S(2)}) collective-permute-start(bf16[2,2,6,48,192]{4,3,2,1,0:T(8,128)(2,1)S(1)} %slice.33), channel_id=1, source_target_pairs={{0,8},{8,16},{16,24},{24,0},{1,9},{9,17},{17,25},{25,1},{2,10},{10... | collective-permute-start | bytes 1327112 | tf_op jit(solution)/shard_map/ppermute | solution.py:394
  253.8 1.1 copy-start.5
  254.9 48.9 %collective-permute-start.7 = (bf16[2,2,6,48,192]{4,3,2,1,0:T(8,128)(2,1)S(1)}, bf16[2,2,6,48,192]{4,3,2,1,0:T(8,128)(2,1)S(1)}, u32[]{:S(2)}, u32[]{:S(2)}) collective-permute-start(bf16[2,2,6,48,192]{4,3,2,1,0:T(8,128)(2,1)S(1)} %slice.34), channel_id=1, source_target_pairs={{0,24},{8,0},{16,8},{24,16},{1,25},{9,1},{17,9},{25,17},{2,26},{10... | collective-permute-start | bytes 1327112 | tf_op jit(solution)/shard_map/ppermute | solution.py:395

commit v2 on v1

--- a/solution.py
+++ b/solution.py
@@ -171,6 +171,7 @@
 AXES = ("band", "px", "py")
 ROW_PAD = 8
 LANES = 128
+CORE_MIDDLE = 0.275
 BF16 = jnp.bfloat16
 F32 = jnp.float32
 LANE_DOT = (((1,), (1,)), ((), ()))
@@ -271,94 +272,142 @@
             out_ref[part, b] = values.reshape(planes, xblock, points).astype(BF16)
 
 
+def pack_rows(first, second):
+    shift = first.shape[1] // 4
+    lane = lax.broadcasted_iota(jnp.int32, (first.shape[0], LANES), 1)
+    tail = jnp.where(lane < shift, first[:, LANES:], pltpu.roll(second[:, LANES:], shift, 1))
+    return jnp.concatenate([first[:, :LANES], second[:, :LANES], tail], 1)
+
+
+def unpack_rows(packed):
+    tail = packed[:, 2 * LANES :]
+    first = jnp.concatenate([packed[:, :LANES], tail], 1)
+    second = jnp.concatenate([packed[:, LANES : 2 * LANES], pltpu.roll(tail, LANES // 2, 1)], 1)
+    return first, second
+
+
+def pack_blocks(values, rows_px):
+    rows = values.shape[0] // (2 * rows_px)
+    halves = values.reshape(rows_px, 2, rows, values.shape[1])
+    first = halves[:, 0].reshape(rows_px * rows, -1)
+    second = halves[:, 1].reshape(rows_px * rows, -1)
+    return pack_rows(first, second).reshape(rows_px, rows, 3 * LANES).astype(BF16)
+
+
 def density_kernel(
-    occ_ref, psi_ref, core_ref, xtab_ref, ytab_ref, ftab_ref, dl_ref, dr_ref,
-    send_ref, rho_ref, gx_ref, gy_ref, gsend_ref, *, bands, planes,
+    scalar_ref, psi_ref, core_ref, xtab_ref, ytab_ref, ftab_ref, dl_ref, send_ref, early_ref, *, bands
 ):
-    points = core_ref.shape[1]
-    total = jnp.zeros((points, points), F32)
-    for b in range(bands):
-        real = psi_ref[0, b, 0]
-        imag = psi_ref[1, b, 0]
-        stacked = jnp.concatenate([real, real, imag, imag], 0)
-        psi = jnp.dot(xtab_ref[...], stacked, preferred_element_type=F32)
-        total = total + occ_ref[b] * (psi[:points] ** 2 + psi[points:] ** 2)
-    rho = total.T + core_ref[0]
-    rho_ref[0] = rho
-    grad_x = mul_right(rho, dr_ref[...])
-    grad_y = mul_left(dl_ref[...], rho)
-    gx_ref[0] = grad_x
-    gy_ref[0] = grad_y
-    rows_px, _, _, y_rows, _ = gsend_ref.shape
-    gsend_ref[:, 0, 0] = grad_x.reshape(rows_px, y_rows, points).astype(BF16)
-    gsend_ref[:, 1, 0] = grad_y.reshape(rows_px, y_rows, points).astype(BF16)
-    spectrum = mul_left(ytab_ref[...], mul_right(rho, ftab_ref[...]))
-    chunks = spectrum.reshape(send_ref.shape[0], ROW_PAD, send_ref.shape[3])
+    rows_px, _, y_rows, points = core_ref.shape
+    spectra = []
+    for k in range(2):
+        total = jnp.zeros((points, points), F32)
+        for b in range(bands):
+            real = psi_ref[0, b, k]
+            imag = psi_ref[1, b, k]
+            stacked = jnp.concatenate([real, real, imag, imag], 0)
+            psi = jnp.dot(xtab_ref[...], stacked, preferred_element_type=F32)
+            total = total + scalar_ref[b] * (psi[:points] ** 2 + psi[points:] ** 2)
+        core = core_ref[:, k].reshape(points, points)
+        rho = total.T + core - scalar_ref[bands]
+        wide = jnp.concatenate([rho, jnp.zeros((points, 2 * LANES - points), F32)], 1)
+        grad_y = mul_left(dl_ref[...], wide)
+        early_ref[:, 0, k] = pack_blocks(wide, rows_px)
+        early_ref[:, 1, k] = pack_blocks(grad_y, rows_px)
+        spectra.append(mul_left(ytab_ref[...], mul_right(rho, ftab_ref[...])))
+    chunks = pack_rows(*spectra)
+    chunks = chunks.reshape(send_ref.shape[0], ROW_PAD, send_ref.shape[3])
     row = lax.broadcasted_iota(jnp.int32, chunks.shape, 1)
     residual = chunks - chunks.astype(BF16).astype(F32)
-    send_ref[:, 0] = jnp.where(row == planes, residual, chunks).astype(BF16)
-
-
-def gather_rows(scratch, first, count):
-    parts = [
-        scratch[h, pl.ds(first, count, stride=ROW_PAD), :] for h in range(scratch.shape[0])
+    send_ref[:, 0] = jnp.where(row == ROW_PAD - 2, residual, chunks).astype(BF16)
+
+
+def load_planes(scratch, first, count):
+    low_a, low_b, tail = [
+        scratch[h, pl.ds(first, count, stride=ROW_PAD), :] for h in range(3)
     ]
-    return jnp.concatenate(parts, 1)
-
-
-def spectral_kernel(
-    place_ref, recv_ref, fwd_ref, inv_ref, der_ref, out_ref, in_scr, h_scr, g_scr, *, planes
-):
+    low = jnp.concatenate([low_a, low_b], 0)
+    high = jnp.concatenate([tail, pltpu.roll(tail, LANES // 2, 1)], 0)
+    return jnp.concatenate([low, high], 1)
+
+
+def spectral_kernel(place_ref, recv_ref, fwd_ref, inv_ref, out_ref, in_scr, out_scr, *, planes):
     points = fwd_ref.shape[0]
-    sources = recv_ref.shape[0]
-    lanes = recv_ref.shape[3]
-    rows = sources * planes * ROW_PAD
-    halves = range(lanes // LANES)
-    arrived = recv_ref[...].astype(F32).reshape(rows, lanes)
-    for h in halves:
-        in_scr[h] = arrived[:, h * LANES : (h + 1) * LANES]
-    h_scr[...] = jnp.zeros_like(h_scr)
-    g_scr[...] = jnp.zeros_like(g_scr)
+    sources, pairs = recv_ref.shape[:2]
+    count = sources * pairs
+    for h in range(3):
+        part = recv_ref[:, :, :, h * LANES : (h + 1) * LANES].astype(F32)
+        in_scr[h] = part.reshape(count * ROW_PAD, LANES)
+    out_scr[...] = jnp.zeros_like(out_scr)
     unit = (2.0 * math.pi / (points * SPACING)) ** 2
-    kz = lax.broadcasted_iota(jnp.int32, (points, lanes), 0)
-    kx = lax.broadcasted_iota(jnp.int32, (points, lanes), 1)
+    kz = lax.broadcasted_iota(jnp.int32, (points, 2 * LANES), 0)
+    kx = lax.broadcasted_iota(jnp.int32, (points, 2 * LANES), 1)
     qz = jnp.minimum(kz, points - kz).astype(F32)
     qx = jnp.minimum(kx, points - kx).astype(F32)
     partial_square = qz * qz + qx * qx
     for j in range(planes):
-        values = gather_rows(in_scr, j, points)
+        values = load_planes(in_scr, j, count)
         if j == 0:
-            values = values + gather_rows(in_scr, planes, points)
+            values = values + load_planes(in_scr, ROW_PAD - 2, count)
         ky = place_ref[0] * planes + j
         qy = jnp.minimum(ky, points - ky).astype(F32)
         squared = unit * (partial_square + qy * qy)
         factor = jnp.where(squared > 0, 4.0 * math.pi / jnp.where(squared > 0, squared, 1.0), 0.0)
         scaled = factor * mul_left(fwd_ref[...], values)
         hartree = mul_left(inv_ref[...], scaled)
-        grad_z = mul_left(der_ref[...], values)
-        for h in halves:
-            h_scr[h, pl.ds(j, points, stride=ROW_PAD), :] = hartree[:, h * LANES : (h + 1) * LANES]
-            g_scr[h, pl.ds(j, points, stride=ROW_PAD), :] = grad_z[:, h * LANES : (h + 1) * LANES]
-    shape = (sources, planes, ROW_PAD, LANES)
-    for h in halves:
-        at = slice(h * LANES, (h + 1) * LANES)
-        out_ref[:, 0, :, :, at] = h_scr[h].reshape(shape).astype(BF16)
-        out_ref[:, 1, :, :, at] = g_scr[h].reshape(shape).astype(BF16)
-
-
-def field_kernel(recv_ref, rho_ref, gx_ref, gy_ref, itab_ref, ytab_ref, send_ref):
-    points = rho_ref.shape[1]
-    rows = recv_ref.shape[0] * ROW_PAD
-    pieces = []
-    for f in range(2):
-        part = recv_ref[:, f, 0].astype(F32).reshape(rows, recv_ref.shape[4]).astype(BF16)
-        part = jnp.concatenate([part, part], 1)
-        part = jnp.dot(part, itab_ref[...], preferred_element_type=F32)
-        pieces.append(mul_left(ytab_ref[...], part))
-    hartree, grad_z = pieces
-    rho = rho_ref[0]
-    grad_x = gx_ref[0]
-    grad_y = gy_ref[0]
+        packed = pack_rows(hartree[:count], hartree[count:])
+        for h in range(3):
+            out_scr[h, pl.ds(j, count, stride=ROW_PAD), :] = packed[:, h * LANES : (h + 1) * LANES]
+    for h in range(3):
+        out_ref[:, :, :, h * LANES : (h + 1) * LANES] = (
+            out_scr[h].reshape(sources, pairs, ROW_PAD, LANES).astype(BF16)
+        )
+
+
+def hartree_kernel(recv_ref, itab_ref, ytab_ref, send_ref):
+    sources, _, pad, lanes = recv_ref.shape
+    arrived = recv_ref[:, 0].astype(F32).reshape(sources * pad, lanes)
+    for k, part in enumerate(unpack_rows(arrived)):
+        part = part.astype(BF16)
+        part = jnp.dot(
+            jnp.concatenate([part, part], 1), itab_ref[...], preferred_element_type=F32
+        )
+        send_ref[:, k] = pack_blocks(mul_left(ytab_ref[...], part), send_ref.shape[0])
+
+
+def grad_z_kernel(place_ref, table_ref, *refs):
+    pieces, (out_ref, in_scr, out_scr) = refs[:-3], refs[-3:]
+    rows = out_ref.shape[2]
+    at = 0
+    for piece in pieces:
+        count = piece.shape[0] * piece.shape[1] * rows
+        in_scr[at : at + count] = piece[...].astype(F32).reshape(count, LANES)
+        at += count
+    depth = at // rows
+    zblock = out_ref.shape[0] * out_ref.shape[1]
+    for r in range(0, rows, 2):
+        values = jnp.concatenate(
+            [in_scr[pl.ds(r + k, depth, stride=rows), :] for k in range(2)], 1
+        ).astype(BF16)
+        values = jnp.concatenate([values, values], 0)
+        slope = jnp.dot(table_ref[0], values, preferred_element_type=F32)
+        for k in range(2):
+            out_scr[pl.ds(r + k, zblock, stride=rows), :] = slope[:, k * LANES : (k + 1) * LANES]
+    out_ref[...] = out_scr[...].reshape(out_ref.shape).astype(BF16)
+
+
+def finish_kernel(place_ref, mean_ref, rho_ref, gy_ref, gz_ref, hartree_ref, dtab_ref, *refs):
+    pot_ref, grad_ref = refs[-2:]
+    planes, rows, lanes = rho_ref.shape[1:]
+    count = planes * rows
+    shape = (planes, rows, lanes)
+    shifted = rho_ref[0].reshape(count, lanes)
+    grad_x = jnp.dot(
+        jnp.concatenate([shifted, shifted], 1), dtab_ref[...], preferred_element_type=F32
+    ).reshape(shape)
+    rho = rho_ref[0].astype(F32) + mean_ref[0]
+    grad_y = gy_ref[0].astype(F32)
+    grad_z = gz_ref[0].astype(F32)
+    hartree = hartree_ref[0].astype(F32)
     cube_root = jnp.exp(jnp.log(rho) * (1.0 / 3.0))
     four_thirds = rho * cube_root
     grad_square = grad_x * grad_x + grad_y * grad_y + grad_z * grad_z
@@ -369,36 +418,43 @@
     potential = hartree - SLATER_COEF * cube_root * (
         4.0 / 3.0 * enhance - 8.0 / 3.0 * reduced * enhance_slope
     )
-    rows_px, _, _, y_rows, _ = send_ref.shape
-    send_ref[:, 0, 0] = potential.reshape(rows_px, y_rows, points).astype(BF16)
-    send_ref[:, 1, 0] = grad_z.reshape(rows_px, y_rows, points).astype(BF16)
-
-
-def place_kernel(place_ref, early_ref, late_ref, *refs):
-    pot_ref, grad_ref = refs[-2:]
-    pot_ref[...] = late_ref[0, 0].astype(F32)
-    grad_ref[0] = early_ref[0, 0].astype(F32)
-    grad_ref[1] = early_ref[0, 1].astype(F32)
-    grad_ref[2] = late_ref[0, 1].astype(F32)
+    store_field(pot_ref, (), potential)
+    store_field(grad_ref, (0,), grad_x)
+    store_field(grad_ref, (1,), grad_y)
+    store_field(grad_ref, (2,), grad_z)
+
+
+def store_field(ref, lead, values):
+    planes, rows, lanes = values.shape
+    half = LANES // 2
+    tail = values[:, :, 2 * LANES :]
+    other = pltpu.roll(tail.reshape(planes * rows, LANES), half, 1).reshape(tail.shape)
+    ref[(*lead, slice(None), slice(0, rows), slice(0, LANES))] = values[:, :, :LANES]
+    ref[(*lead, slice(None), slice(rows, 2 * rows), slice(0, LANES))] = (
+        values[:, :, LANES : 2 * LANES]
+    )
+    ref[(*lead, slice(None), slice(0, rows), slice(LANES, LANES + half))] = tail[:, :, :half]
+    ref[(*lead, slice(None), slice(rows, 2 * rows), slice(LANES, LANES + half))] = (
+        other[:, :, :half]
+    )
 
 
 def ring_gather(values, axis):
     size = lax.axis_size(axis)
     up = [(i, (i + 1) % size) for i in range(size)]
     down = [(i, (i - 1) % size) for i in range(size)]
-    found = {0: values}
+    found = [(0, 0, values)]
     from_below = from_above = values
     for step in range(1, size // 2 + 1):
         if 2 * step == size:
             cut = values.shape[0] // 2
-            low = lax.ppermute(from_below[:cut], axis, up)
-            high = lax.ppermute(from_above[cut:], axis, down)
-            found[step] = jnp.concatenate([low, high], 0)
+            found.append((step, 0, lax.ppermute(from_below[:cut], axis, up)))
+            found.append((step, cut, lax.ppermute(from_above[cut:], axis, down)))
         else:
             from_below = lax.ppermute(from_below, axis, up)
             from_above = lax.ppermute(from_above, axis, down)
-            found[size - step] = from_below
-            found[step] = from_above
+            found.append((size - step, 0, from_below))
+            found.append((step, 0, from_above))
     return found
 
 
@@ -439,7 +495,13 @@
     occ_mid = (occ - occ_high).astype(BF16).astype(F32)
     occ_low = occ - occ_high - occ_mid
     lane = jnp.arange(columns)[None, :]
-    extra = jnp.concatenate([occ_high, jnp.where(lane < columns // 2, occ_mid, occ_low)], 0)
+    norm = jnp.sum(source.astype(F32) ** 2) * occ
+    norm_high = norm.astype(BF16).astype(F32)
+    quarter = columns // 4
+    numbers = jnp.where(lane < 2 * quarter, occ_low, norm_high)
+    numbers = jnp.where(lane < quarter, occ_mid, numbers)
+    numbers = jnp.where(lane < 3 * quarter, numbers, norm - norm_high)
+    extra = jnp.concatenate([occ_high, numbers], 0)
     zeros = jnp.zeros((6, columns), F32)
     extra = jnp.concatenate([zeros, extra, zeros, own], 0)
     row = lax.broadcasted_iota(jnp.int32, waves.shape, 1)
@@ -447,10 +509,14 @@
     sticks = lax.all_to_all(waves, AXES, split_axis=0, concat_axis=0, tiled=True)
     sticks = sticks.reshape(bands, rows_px, rows_py, 16, columns)
     core = lax.dynamic_slice_in_dim(core_density, band * zshare, zshare, 0)
-    core = lax.all_to_all(core, "px", split_axis=0, concat_axis=1, tiled=True)
+    core = core.reshape(rows_px, planes, y_rows, points)
+    core = lax.all_to_all(core, "px", split_axis=0, concat_axis=0, tiled=True)
     occ_all = sticks[:, 0, 0, 6, 0].astype(F32) + (
-        sticks[:, 0, 0, 7, 0].astype(F32) + sticks[:, 0, 0, 7, columns - 1].astype(F32)
-    )
+        sticks[:, 0, 0, 7, 0].astype(F32) + sticks[:, 0, 0, 7, quarter].astype(F32)
+    )
+    norms = sticks[:, :, :, 7, 2 * quarter].astype(F32) + sticks[:, :, :, 7, columns - 1].astype(F32)
+    mean = (jnp.sum(norms) + CORE_MIDDLE).reshape(1)
+    scalars = jnp.concatenate([occ_all, mean])
 
     cos_high, cos_low = split_table(cosine)
     sin_high, sin_low = split_table(sine)
@@ -472,13 +538,13 @@
 
     basis = real_basis(points)
     slope = derivative(points)
-    lanes = -(-points // LANES) * LANES
+    lanes = 2 * LANES
     basis_lanes = np.zeros((points, lanes))
     basis_lanes[:, :points] = basis.T
     padded = np.zeros((devices, ROW_PAD, points))
     padded[:, :planes] = basis.reshape(devices, planes, points)
     inverse_pad = padded.reshape(devices * ROW_PAD, points).T.copy()
-    padded[:, planes] = padded[:, 0]
+    padded[:, ROW_PAD - 2] = padded[:, 0]
     forward_pad = padded.reshape(devices * ROW_PAD, points)
     x_table = np.concatenate(
         [
@@ -487,97 +553,148 @@
         ],
         0,
     )
-    tables = [
-        x_table, left3(forward_pad), right3(basis_lanes), left3(slope), right3(slope.T),
-    ]
-    whole = lambda t: pl.BlockSpec(t.shape, lambda i: (0,) * t.ndim)
-    plane_spec = pl.BlockSpec((1, points, points), lambda i: (i, 0, 0))
-    plane_shape = jax.ShapeDtypeStruct((planes, points, points), F32)
-    pair_spec = pl.BlockSpec((rows_px, 2, 1, y_rows, points), lambda i: (0, 0, i, 0, 0))
-    pair_shape = jax.ShapeDtypeStruct((rows_px, 2, planes, y_rows, points), BF16)
-    sent, rho, grad_x, grad_y, early = pl.pallas_call(
-        lambda *refs: density_kernel(*refs, bands=bands, planes=planes),
-        grid=(planes,),
+    tables = [x_table, left3(forward_pad), right3(basis_lanes), left3(slope)]
+    whole = lambda t: pl.BlockSpec(t.shape, lambda *i: (0,) * t.ndim)
+    in_smem = pl.BlockSpec(memory_space=pltpu.SMEM)
+    in_vmem = pl.BlockSpec(memory_space=pltpu.VMEM)
+    pairs = planes // 2
+    half_rows = y_rows // 2
+    width = 3 * LANES
+    chunk_spec = pl.BlockSpec((devices, 1, ROW_PAD, width), lambda i: (0, i, 0, 0))
+    chunk_shape = jax.ShapeDtypeStruct((devices, pairs, ROW_PAD, width), BF16)
+    spread, early = pl.pallas_call(
+        lambda *refs: density_kernel(*refs, bands=bands),
+        grid=(pairs,),
         in_specs=[
-            pl.BlockSpec(memory_space=pltpu.SMEM),
-            pl.BlockSpec((2, bands, 1, points, points), lambda i: (0, 0, i, 0, 0)),
-            plane_spec,
+            in_smem,
+            pl.BlockSpec((2, bands, 2, points, points), lambda i: (0, 0, i, 0, 0)),
+            pl.BlockSpec((rows_px, 2, y_rows, points), lambda i: (0, i, 0, 0)),
         ] + [whole(t) for t in tables],
         out_specs=[
-            pl.BlockSpec((devices, 1, ROW_PAD, lanes), lambda i: (0, i, 0, 0)),
-            plane_spec, plane_spec, plane_spec, pair_spec,
+            chunk_spec,
+            pl.BlockSpec((rows_px, 2, 2, half_rows, width), lambda i: (0, 0, i, 0, 0)),
         ],
         out_shape=[
-            jax.ShapeDtypeStruct((devices, planes, ROW_PAD, lanes), BF16),
-            plane_shape, plane_shape, plane_shape, pair_shape,
+            chunk_shape,
+            jax.ShapeDtypeStruct((rows_px, 2, planes, half_rows, width), BF16),
         ],
         name="density",
-    )(occ_all, psi_y, core, *tables)
-
-    spread = lax.all_to_all(sent, AXES, split_axis=0, concat_axis=0, tiled=True)
+    )(scalars, psi_y, core, *tables)
+
+    spread = lax.all_to_all(spread, AXES, split_axis=0, concat_axis=0, tiled=True)
     early = lax.all_to_all(early, "px", split_axis=0, concat_axis=0, tiled=True)
-    early = ring_gather(early, "band")
+    rho_pieces = ring_gather(early[:, 0], "band")
+    slope_pieces = ring_gather(early[:, 1], "band")
+    swap = [(i, (i + rows_py // 2) % rows_py) for i in range(rows_py)]
+    other_pieces = [lax.ppermute(piece, "py", swap) for _, _, piece in rho_pieces]
 
     place = ((band * rows_px + px) * rows_py + py).reshape(1)
-    order = z_order.reshape(-1)
-    z_tables = [
-        left3(basis[:, order]), left3(basis.T[order]), left3(slope[order][:, order]),
-    ]
-    rows = points * ROW_PAD
+    order = np.concatenate([z_order[:, ::2].reshape(-1), z_order[:, 1::2].reshape(-1)])
+    z_tables = [left3(basis[:, order]), left3(basis.T[order])]
     spread = pl.pallas_call(
         lambda *refs: spectral_kernel(*refs, planes=planes),
-        in_specs=[pl.BlockSpec(memory_space=pltpu.SMEM)]
-        + [pl.BlockSpec(memory_space=pltpu.VMEM)] * 4,
-        out_specs=pl.BlockSpec(memory_space=pltpu.VMEM),
-        out_shape=jax.ShapeDtypeStruct((devices, 2, planes, ROW_PAD, lanes), BF16),
-        scratch_shapes=[pltpu.VMEM((lanes // LANES, rows, LANES), F32)] * 3,
+        in_specs=[in_smem, in_vmem, in_vmem, in_vmem],
+        out_specs=in_vmem,
+        out_shape=chunk_shape,
+        scratch_shapes=[pltpu.VMEM((3, devices * pairs * ROW_PAD, LANES), F32)] * 2,
         name="spectral",
     )(place, spread, *z_tables)
     spread = lax.all_to_all(spread, AXES, split_axis=0, concat_axis=0, tiled=True)
 
-    basis_high, basis_low = split_table(basis_lanes.T)
-    back_tables = [np.concatenate([basis_high, basis_low], 0), left3(inverse_pad)]
-    late = pl.pallas_call(
-        field_kernel,
-        grid=(planes,),
-        in_specs=[
-            pl.BlockSpec((devices, 2, 1, ROW_PAD, lanes), lambda i: (0, 0, i, 0, 0)),
-            plane_spec, plane_spec, plane_spec,
-        ] + [whole(t) for t in back_tables],
-        out_specs=pair_spec,
-        out_shape=pair_shape,
-        name="fields",
-    )(spread, rho, grad_x, grad_y, *back_tables)
-    late = lax.all_to_all(late, "px", split_axis=0, concat_axis=0, tiled=True)
-    late = ring_gather(late, "band")
-
+    back = np.zeros((lanes, lanes))
+    back[:points, :points] = basis
+    back_tables = [np.concatenate(split_table(back), 0), left3(inverse_pad)]
+    hartree = pl.pallas_call(
+        hartree_kernel,
+        grid=(pairs,),
+        in_specs=[chunk_spec] + [whole(t) for t in back_tables],
+        out_specs=pl.BlockSpec((rows_px, 2, half_rows, width), lambda i: (0, i, 0, 0)),
+        out_shape=jax.ShapeDtypeStruct((rows_px, planes, half_rows, width), BF16),
+        name="hartree",
+    )(spread, *back_tables)
+    hartree = lax.all_to_all(hartree, "px", split_axis=0, concat_axis=0, tiled=True)
+    hartree_pieces = ring_gather(hartree, "band")
+
+    inside = np.arange(zshare).reshape(rows_px, planes)
+    depth_tables = []
+    for b in range(bands):
+        rows = np.concatenate([(b + t) % bands * zshare + inside.reshape(-1) for t in range(bands)])
+        cols = np.concatenate(
+            [
+                (((b + t) % bands * zshare) + inside[first : first + piece.shape[0]]).reshape(-1)
+                for t, first, piece in rho_pieces
+            ]
+        )
+        cols = np.concatenate([cols, cols + zblock])
+        high, low = split_table(slope[rows][:, cols])
+        depth_tables.append(np.concatenate([high, low], 1))
+    depth_tables = np.stack(depth_tables)
+    gathered = [piece for _, _, piece in rho_pieces] + other_pieces
+    depth_rows = bands * rows_px
+    grad_z = pl.pallas_call(
+        grad_z_kernel,
+        grid_spec=pltpu.PrefetchScalarGridSpec(
+            num_scalar_prefetch=1,
+            grid=(3,),
+            in_specs=[pl.BlockSpec((1,) + depth_tables.shape[1:], lambda i, s: (s[0], 0, 0))]
+            + [
+                pl.BlockSpec(piece.shape[:3] + (LANES,), lambda i, s: (0, 0, 0, i))
+                for piece in gathered
+            ],
+            out_specs=pl.BlockSpec(
+                (depth_rows, planes, half_rows, LANES), lambda i, s: (0, 0, 0, i)
+            ),
+            scratch_shapes=[
+                pltpu.VMEM((points * half_rows, LANES), F32),
+                pltpu.VMEM((zblock * half_rows, LANES), F32),
+            ],
+        ),
+        out_shape=jax.ShapeDtypeStruct((depth_rows, planes, half_rows, width), BF16),
+        name="grad_z",
+    )(band.reshape(1), depth_tables, *gathered)
+
+    packed = np.zeros((width, width))
+    spots = [
+        np.where(np.arange(points) < LANES, np.arange(points), np.arange(points) + LANES),
+        np.where(
+            np.arange(points) < LANES, np.arange(points) + LANES, np.arange(points) + LANES * 3 // 2
+        ),
+    ]
+    for spot in spots:
+        packed[np.ix_(spot, spot)] = slope.T
+    packed_table = np.concatenate(split_table(packed), 0)
     out_shape = [
         jax.ShapeDtypeStruct((zblock, y_rows, points), F32),
         jax.ShapeDtypeStruct((3, zblock, y_rows, points), F32),
     ]
     results = []
-    for shift in range(bands):
-        index = ((band + shift) % bands).reshape(1)
-        piece = pl.BlockSpec((1, 2, planes, y_rows, points), lambda i, s: (i, 0, 0, 0, 0))
+    for number, (shift, first, piece) in enumerate(hartree_pieces):
+        spot = jnp.stack([(band + shift) % bands * rows_px + first])
+        block = (1, planes, half_rows, width)
+        piece_spec = pl.BlockSpec(block, lambda i, s: (i, 0, 0, 0))
+        at = shift * rows_px + first
         results = pl.pallas_call(
-            place_kernel,
+            finish_kernel,
             grid_spec=pltpu.PrefetchScalarGridSpec(
                 num_scalar_prefetch=1,
-                grid=(rows_px,),
-                in_specs=[piece, piece] + [pl.BlockSpec(memory_space=pl.ANY)] * len(results),
+                grid=(piece.shape[0],),
+                in_specs=[
+                    in_smem, piece_spec, piece_spec,
+                    pl.BlockSpec(block, lambda i, s, at=at: (at + i, 0, 0, 0)),
+                    piece_spec, whole(packed_table),
+                ] + [pl.BlockSpec(memory_space=pl.ANY)] * len(results),
                 out_specs=[
-                    pl.BlockSpec(
-                        (planes, y_rows, points), lambda i, s: (s[0] * rows_px + i, 0, 0)
-                    ),
-                    pl.BlockSpec(
-                        (3, planes, y_rows, points), lambda i, s: (0, s[0] * rows_px + i, 0, 0)
-                    ),
+                    pl.BlockSpec((planes, y_rows, points), lambda i, s: (s[0] + i, 0, 0)),
+                    pl.BlockSpec((3, planes, y_rows, points), lambda i, s: (0, s[0] + i, 0, 0)),
                 ],
             ),
             out_shape=out_shape,
-            input_output_aliases={3: 0, 4: 1} if results else {},
-            name="place",
-        )(index, early[shift], late[shift], *results)
+            input_output_aliases={7: 0, 8: 1} if results else {},
+            name="finish",
+        )(
+            spot, mean, rho_pieces[number][2], slope_pieces[number][2], grad_z, piece,
+            packed_table, *results,
+        )
     return tuple(results)
 
 
@@ -585,7 +702,8 @@
     points = orbitals.shape[2] // 2
     devices = lax.axis_size("band") * lax.axis_size("px") * lax.axis_size("py")
     planes = points // devices
-    whole_planes = points % (2 * devices) == 0 and planes < 7 and points <= 256
+    whole_planes = points % (2 * devices) == 0 and planes < 7 and points == 3 * LANES // 2
+    whole_planes = whole_planes and lax.axis_size("py") == 2
     if whole_planes and orbitals.shape[0] == 1 and orbitals.shape[1] % 128 == 0:
         return slab_body(orbitals, occupations, stick_map, core_density)
     return pencil_body(orbitals, occupations, stick_map, core_density)

time: 316 us -> 237 us (0.75)
  waiting for transfers between devices: 122 us -> 67.2 us
  blocking collectives: 41.1 us -> 19.7 us
  starting transfers between devices: 78.5 us -> 69.8 us
  Pallas kernels: 52.3 us -> 58.3 us
    ppermute x4 -> x11, starting transfers between devices: 50.3 us -> 20 us  [the longest x3 7.8 us: ring_gather(): found.append((step, 0, lax.ppermute(from_below[:cut], axis, up)))]
    all_to_all x3, waiting for transfers between devices: 38.1 us -> 16.4 us  [the longest x1 13.2 us: slab_body(): lax.all_to_all(spread, AXES, split_axis=0, concat_axis=0, tiled=True)]
    all_to_all x1, blocking collectives: 41.1 us -> 19.7 us  [slab_body(): lax.all_to_all(spread, AXES, split_axis=0, concat_axis=0, tiled=True)]
    ppermute x2 -> x3, waiting for transfers between devices: 33.9 us -> 12.8 us  [ring_gather(): from_below = lax.ppermute(from_below, axis, up)]
    ppermute x4 -> x11, waiting for transfers between devices: 35.9 us -> 22.9 us  [the longest x3 10.5 us: ring_gather(): found.append((step, cut, lax.ppermute(from_above[cut:], axis, down)))]
    ppermute x2 -> x3, starting transfers between devices: 1.34 us -> 12.6 us  [ring_gather(): from_below = lax.ppermute(from_below, axis, up)]
    ppermute x2 -> x3, starting transfers between devices: 6.36 us -> 16.5 us  [ring_gather(): from_above = lax.ppermute(from_above, axis, down)]
    pallas_call x6 -> x8, Pallas kernels: 38 us -> 45.9 us  [the longest x5 23.4 us: slab_body(): pl.pallas_call(finish_kernel, grid_spec=pltpu.PrefetchScalarGridSpec(num_...]
  transfers between devices with their start and end apart: 13 -> 22, of which waited for: 12 -> 9; matrix products, arithmetic and copies ran while one was open for 3% -> 4% of each run, Pallas kernels for 8% -> 18%
where the time goes in v2:
time: 237 us; the launch traced here: 236 us
  starting transfers between devices  69.8 us (29%)
  waiting for transfers between devices  67.2 us (28%)
  Pallas kernels  58.3 us (25%)
  blocking collectives  19.7 us (8%)
  local copies, waits for them, and re-layouts  8.83 us (4%)
  other arithmetic  6.25 us (3%)
  between operations  2.89 us (1%)
  matrix products  2.55 us (1%)
    pallas_call x5, Pallas kernels, slab_body(): pl.pallas_call(finish_kernel, grid_spec=pltpu.PrefetchScalarGridSpec(num_...  23.4 us
    all_to_all x1, blocking collectives, slab_body(): lax.all_to_all(spread, AXES, split_axis=0, concat_axis=0, tiled=True)  19.7 us
    ppermute x3, starting transfers between devices, ring_gather(): from_above = lax.ppermute(from_above, axis, down)  16.5 us
    all_to_all x1, waiting for transfers between devices, slab_body(): lax.all_to_all(spread, AXES, split_axis=0, concat_axis=0, tiled=True)  13.2 us
    ppermute x3, waiting for transfers between devices, ring_gather(): from_below = lax.ppermute(from_below, axis, up)  12.8 us
    ppermute x3, starting transfers between devices, ring_gather(): from_below = lax.ppermute(from_below, axis, up)  12.6 us
    pallas_call x1, Pallas kernels, slab_body(): pl.pallas_call(lambda *refs: density_kernel(*refs, bands=bands), grid=(pa...  12.3 us
    ppermute x3, waiting for transfers between devices, ring_gather(): found.append((step, cut, lax.ppermute(from_above[cut:], axis, down)))  10.5 us
  transfers between devices with their start and end apart: 22, of which 9 were waited for; matrix products, arithmetic and copies ran while one was open for 4% of the time, Pallas kernels for 18%

profile of v2, /device:TPU:0, one launch (start us, length us, event | category | flops | bytes accessed | tf_op | source)
XLA Modules:
  0.0 235.5 jit_solution(14239852670035661037)
XLA Ops:
  7.7 7.3 %all-to-all-start = ((bf16[32,16,128]{2,1,0:T(8,128)(2,1)}), bf16[32,16,128]{2,1,0:T(8,128)(2,1)S(1)}, u32[]{:S(2)}, u32[]{:S(2)}) async-start(bf16[32,16,128]{2,1,0:T(8,128)(2,1)} %select_convert_fusion), calls=%async_computation | async-start | bytes 262144 | tf_op jit(solution)/shard_map/all_to_all | solution.py:509
  17.4 6.2 %all-to-all-done = bf16[32,16,128]{2,1,0:T(8,128)(2,1)S(1)} async-done(((bf16[32,16,128]{2,1,0:T(8,128)(2,1)}), bf16[32,16,128]{2,1,0:T(8,128)(2,1)S(1)}, u32[]{:S(2)}, u32[]{:S(2)}) %all-to-all-start) | async-done | bytes 131104 | tf_op jit(solution)/shard_map/all_to_all | solution.py:509
  23.6 3.5 %all-to-all-start.1 = ((f32[4,6,48,192]{3,2,1,0:T(8,128)}), f32[4,6,48,192]{3,2,1,0:T(8,128)S(1)}, u32[]{:S(2)}, u32[]{:S(2)}) async-start(f32[4,6,48,192]{3,2,1,0:T(8,128)} %bitcast.12), calls=%async_computation.1 | async-start | bytes 2359296 | tf_op jit(solution)/shard_map/all_to_all | solution.py:513
  27.2 8.7 %planes.1.refs_1_ = bf16[2,4,6,192,192]{4,3,2,1,0:T(8,128)(2,1)} custom-call(bf16[4,4,2,16,128]{4,3,2,1,0:T(8,128)(2,1)} %bitcast.35, bf16[768,192]{1,0:T(8,128)(2,1)} %constant.107.clone.refs_1_), custom_call_target="tpu_custom_call" | custom-call | tf_op jit(solution)/shard_map/planes/pallas_call | solution.py:524
  44.0 12.3 %density.1 = (bf16[32,3,8,384]{3,2,1,0:T(8,128)(2,1)}, bf16[4,2,6,24,384]{4,3,2,1,0:T(8,128)(2,1)}) custom-call(f32[5]{0:T(128)} %pad_maximum_fusion.refs_0_, bf16[2,4,6,192,192]{4,3,2,1,0:T(8,128)(2,1)} %planes.1.refs_1_, f32[4,6,48,192]{3,2,1,0:T(8,128)} %copy-done, bf16[384,768]{1,0:T(8,128)(2,1)} %constant.108.clone.refs_3_, ...), custom_call_target="tpu_custom_call" | custom-call | tf_op jit(solution)/shard_map/density/pallas_call | solution.py:565
  56.2 19.7 %all_to_all.30.refs_1_ = bf16[32,3,8,384]{3,2,1,0:T(8,128)(2,1)} all-to-all(bf16[32,3,8,384]{3,2,1,0:T(8,128)(2,1)} %get-tuple-element.13), channel_id=1, replica_groups=mesh['band'=4,'px'=4,'py'=2] {'band','px','py'}, dimensions={0} | all-to-all | bytes 1179648 | tf_op jit(solution)/shard_map/all_to_all | solution.py:584
  75.9 3.5 %all-to-all-start.2 = ((bf16[4,2,6,24,384]{4,3,2,1,0:T(8,128)(2,1)}), bf16[4,2,6,24,384]{4,3,2,1,0:T(8,128)(2,1)S(1)}, u32[]{:S(2)}, u32[]{:S(2)}) async-start(bf16[4,2,6,24,384]{4,3,2,1,0:T(8,128)(2,1)} %get-tuple-element.12), calls=%async_computation.2 | async-start | bytes 1769472 | tf_op jit(solution)/shard_map/all_to_all | solution.py:585
  79.4 3.8 %spectral.1 = bf16[32,3,8,384]{3,2,1,0:T(8,128)(2,1)} custom-call(s32[1]{0:T(128)} %bitcast.16.refs_0_, bf16[32,3,8,384]{3,2,1,0:T(8,128)(2,1)} %all_to_all.30.refs_1_, bf16[192,576]{1,0:T(8,128)(2,1)} %constant.112.clone.refs_2_, bf16[192,576]{1,0:T(8,128)(2,1)} %constant.113.clone.refs_3_), custom_call_target="tpu_custom_call" | custom-call | tf_op jit(solution)/shard_map/spectral/pallas_call | solution.py:594
  83.2 8.9 %all-to-all-done.2 = bf16[4,2,6,24,384]{4,3,2,1,0:T(8,128)(2,1)S(1)} async-done(((bf16[4,2,6,24,384]{4,3,2,1,0:T(8,128)(2,1)}), bf16[4,2,6,24,384]{4,3,2,1,0:T(8,128)(2,1)S(1)}, u32[]{:S(2)}, u32[]{:S(2)}) %all-to-all-start.2) | async-done | bytes 884768 | tf_op jit(solution)/shard_map/all_to_all | solution.py:585
  95.1 3.7 %collective-permute-start = (bf16[4,6,24,384]{3,2,1,0:T(8,128)(2,1)S(1)}, bf16[4,6,24,384]{3,2,1,0:T(8,128)(2,1)S(1)}, u32[]{:S(2)}, u32[]{:S(2)}) collective-permute-start(bf16[4,6,24,384]{3,2,1,0:T(8,128)(2,1)S(1)} %get-tuple-element.23.refs_0_.rho_ref), channel_id=1, source_target_pairs={{0,24},{8,0},{16,8},{24,16},{1,25},{9,1},{17,9},{25,17},{2,26},{10... | collective-permute-start | bytes 1327112 | tf_op jit(solution)/shard_map/ppermute | solution.py:455
  98.8 13.2 %all-to-all-done.4.recv_ref = bf16[32,3,8,384]{3,2,1,0:T(8,128)(2,1)S(1)} async-done(((bf16[32,3,8,384]{3,2,1,0:T(8,128)(2,1)}), bf16[32,3,8,384]{3,2,1,0:T(8,128)(2,1)S(1)}, u32[]{:S(2)}, u32[]{:S(2)}) %all-to-all-start.4) | async-done | bytes 589856 | tf_op jit(solution)/shard_map/all_to_all | solution.py:602
  112.8 4.3 %hartree.1 = bf16[4,6,24,384]{3,2,1,0:T(8,128)(2,1)} custom-call(bf16[32,3,8,384]{3,2,1,0:T(8,128)(2,1)} %copy-done.4, bf16[512,256]{1,0:T(8,128)(2,1)} %constant.114.clone.itab_ref, bf16[192,768]{1,0:T(8,128)(2,1)} %constant.115.clone.ytab_ref), custom_call_target="tpu_custom_call" | custom-call | tf_op jit(solution)/shard_map/hartree/pallas_call | solution.py:607
  117.1 3.5 %all-to-all-start.5 = ((bf16[4,6,24,384]{3,2,1,0:T(8,128)(2,1)}), bf16[4,6,24,384]{3,2,1,0:T(8,128)(2,1)S(1)}, u32[]{:S(2)}, u32[]{:S(2)}) async-start(bf16[4,6,24,384]{3,2,1,0:T(8,128)(2,1)} %hartree.1), calls=%async_computation.5 | async-start | bytes 884736 | tf_op jit(solution)/shard_map/all_to_all | solution.py:615
  120.5 7.4 %collective-permute-start.4 = (bf16[4,6,24,384]{3,2,1,0:T(8,128)(2,1)S(1)}, bf16[4,6,24,384]{3,2,1,0:T(8,128)(2,1)S(1)}, u32[]{:S(2)}, u32[]{:S(2)}) collective-permute-start(bf16[4,6,24,384]{3,2,1,0:T(8,128)(2,1)S(1)} %get-tuple-element.23.refs_0_.rho_ref), channel_id=1, source_target_pairs={{0,8},{8,16},{16,24},{24,0},{1,9},{9,17},{17,25},{25,1},{2,10},{10... | collective-permute-start | bytes 1327112 | tf_op jit(solution)/shard_map/ppermute | solution.py:454
  135.8 6.0 %collective-permute-done.4.refs_1_.rho_ref = bf16[4,6,24,384]{3,2,1,0:T(8,128)(2,1)S(1)} collective-permute-done((bf16[4,6,24,384]{3,2,1,0:T(8,128)(2,1)S(1)}, bf16[4,6,24,384]{3,2,1,0:T(8,128)(2,1)S(1)}, u32[]{:S(2)}, u32[]{:S(2)}) %collective-permute-start.4) | collective-permute-done | bytes 442400 | tf_op jit(solution)/shard_map/ppermute | solution.py:454
  144.5 6.8 %collective-permute-done.13.gy_ref = bf16[4,6,24,384]{3,2,1,0:T(8,128)(2,1)S(1)} collective-permute-done((bf16[4,6,24,384]{3,2,1,0:T(8,128)(2,1)S(1)}, bf16[4,6,24,384]{3,2,1,0:T(8,128)(2,1)S(1)}, u32[]{:S(2)}, u32[]{:S(2)}) %collective-permute-start.13) | collective-permute-done | bytes 442400 | tf_op jit(solution)/shard_map/ppermute | solution.py:454
  151.3 11.8 %collective-permute-start.11 = (bf16[4,6,24,384]{3,2,1,0:T(8,128)(2,1)S(1)}, bf16[4,6,24,384]{3,2,1,0:T(8,128)(2,1)S(1)}, u32[]{:S(2)}, u32[]{:S(2)}) collective-permute-start(bf16[4,6,24,384]{3,2,1,0:T(8,128)(2,1)S(1)} %all-to-all-done.5.hartree_ref), channel_id=1, source_target_pairs={{0,24},{8,0},{16,8},{24,16},{1,25},{9,1},{17,9},{25,17},{2,26},{10... | collective-permute-start | bytes 1327112 | tf_op jit(solution)/shard_map/ppermute | solution.py:455
  164.7 10.5 %collective-permute-done.1.refs_4_.rho_ref = bf16[2,6,24,384]{3,2,1,0:T(8,128)(2,1)S(1)} collective-permute-done((bf16[2,6,24,384]{3,2,1,0:T(8,128)(2,1)S(1)}, bf16[2,6,24,384]{3,2,1,0:T(8,128)(2,1)S(1)}, u32[]{:S(2)}, u32[]{:S(2)}) %collective-permute-start.1) | collective-permute-done | bytes 221216 | tf_op jit(solution)/shard_map/ppermute | solution.py:452
  183.4 9.6 %collective-permute-done.10.refs_9_ = bf16[2,6,24,384]{3,2,1,0:T(8,128)(2,1)S(1)} collective-permute-done((bf16[2,6,24,384]{3,2,1,0:T(8,128)(2,1)S(1)}, bf16[2,6,24,384]{3,2,1,0:T(8,128)(2,1)S(1)}, u32[]{:S(2)}, u32[]{:S(2)}) %collective-permute-start.10) | collective-permute-done | bytes 221216 | tf_op jit(solution)/shard_map/ppermute | solution.py:589
  193.0 5.0 %collective-permute-start.14 = (bf16[2,6,24,384]{3,2,1,0:T(8,128)(2,1)}, bf16[2,6,24,384]{3,2,1,0:T(8,128)(2,1)}, u32[]{:S(2)}, u32[]{:S(2)}) collective-permute-start(bf16[2,6,24,384]{3,2,1,0:T(8,128)(2,1)} %slice.63), channel_id=1, source_target_pairs={{0,8},{8,16},{16,24},{24,0},{1,9},{9,17},{17,25},{25,1},{2,10},{10... | collective-permute-start | bytes 663560 | tf_op jit(solution)/shard_map/ppermute | solution.py:451
  205.5 5.9 %grad_z.1.gz_ref = bf16[16,6,24,384]{3,2,1,0:T(8,128)(2,1)} custom-call(s32[1]{0:T(128)} %bitcast.15.place_ref, bf16[4,96,384]{2,1,0:T(8,128)(2,1)} %constant.116.clone.table_ref, bf16[4,6,24,384]{3,2,1,0:T(8,128)(2,1)} %copy-done.1, bf16[4,6,24,384]{3,2,1,0:T(8,128)(2,1)} %copy-done.3, bf16[4,6,24,384]{3,2,1,0:T(8,128)(2,1)} %copy-done.2, ...), custom_call_target="tpu_custom_call" | custom-call | tf_op jit(solution)/shard_map/grad_z/pallas_call | solution.py:634
  211.4 5.6 %finish.5 = (f32[96,48,192]{2,1,0:T(8,128)}, f32[3,96,48,192]{3,2,1,0:T(8,128)}) custom-call(s32[1]{0:T(128)} %bitcast.20.place_ref, f32[1]{0:T(128)} %bitcast.11.mean_ref, bf16[4,6,24,384]{3,2,1,0:T(8,128)(2,1)} %copy-done.1, bf16[4,6,24,384]{3,2,1,0:T(8,128)(2,1)} %copy-done.5, bf16[16,6,24,384]{3,2,1,0:T(8,128)(2,1)} %grad_z.1.gz_ref, ...), custom_call_target="tpu_custom_call" | custom-call | tf_op jit(solution)/shard_map/finish/pallas_call | solution.py:676
  217.0 5.5 %finish.6 = (f32[96,48,192]{2,1,0:T(8,128)}, f32[3,96,48,192]{3,2,1,0:T(8,128)}) custom-call(s32[1]{0:T(128)} %bitcast.19.place_ref, f32[1]{0:T(128)} %bitcast.11.mean_ref, bf16[4,6,24,384]{3,2,1,0:T(8,128)(2,1)} %copy-done.3, bf16[4,6,24,384]{3,2,1,0:T(8,128)(2,1)} %copy-done.8, ...), custom_call_target="tpu_custom_call", output_to_operand_aliasing={{0}: (7, {}), {1}: (8, {})} | custom-call | tf_op jit(solution)/shard_map/finish/pallas_call | solution.py:676
  222.5 5.5 %finish.7 = (f32[96,48,192]{2,1,0:T(8,128)}, f32[3,96,48,192]{3,2,1,0:T(8,128)}) custom-call(s32[1]{0:T(128)} %bitcast.18.place_ref, f32[1]{0:T(128)} %bitcast.11.mean_ref, bf16[4,6,24,384]{3,2,1,0:T(8,128)(2,1)} %copy-done.2, bf16[4,6,24,384]{3,2,1,0:T(8,128)(2,1)} %copy-done.7, ...), custom_call_target="tpu_custom_call", output_to_operand_aliasing={{0}: (7, {}), {1}: (8, {})} | custom-call | tf_op jit(solution)/shard_map/finish/pallas_call | solution.py:676
  (89 shorter events, 54.8 us)
Async XLA Ops:
  7.7 15.9 %all-to-all-start = ((bf16[32,16,128]{2,1,0:T(8,128)(2,1)}), bf16[32,16,128]{2,1,0:T(8,128)(2,1)S(1)}, u32[]{:S(2)}, u32[]{:S(2)}) async-start(bf16[32,16,128]{2,1,0:T(8,128)(2,1)} %select_convert_fusion), calls=%async_computation | async-start | bytes 262144 | tf_op jit(solution)/shard_map/all_to_all | solution.py:509
  23.6 19.3 %all-to-all-start.1 = ((f32[4,6,48,192]{3,2,1,0:T(8,128)}), f32[4,6,48,192]{3,2,1,0:T(8,128)S(1)}, u32[]{:S(2)}, u32[]{:S(2)}) async-start(f32[4,6,48,192]{3,2,1,0:T(8,128)} %bitcast.12), calls=%async_computation.1 | async-start | bytes 2359296 | tf_op jit(solution)/shard_map/all_to_all | solution.py:513
  75.9 16.2 %all-to-all-start.2 = ((bf16[4,2,6,24,384]{4,3,2,1,0:T(8,128)(2,1)}), bf16[4,2,6,24,384]{4,3,2,1,0:T(8,128)(2,1)S(1)}, u32[]{:S(2)}, u32[]{:S(2)}) async-start(bf16[4,2,6,24,384]{4,3,2,1,0:T(8,128)(2,1)} %get-tuple-element.12), calls=%async_computation.2 | async-start | bytes 1769472 | tf_op jit(solution)/shard_map/all_to_all | solution.py:585
  92.0 19.9 %all-to-all-start.4 = ((bf16[32,3,8,384]{3,2,1,0:T(8,128)(2,1)}), bf16[32,3,8,384]{3,2,1,0:T(8,128)(2,1)S(1)}, u32[]{:S(2)}, u32[]{:S(2)}) async-start(bf16[32,3,8,384]{3,2,1,0:T(8,128)(2,1)} %spectral.1), calls=%async_computation.4 | async-start | bytes 1179648 | tf_op jit(solution)/shard_map/all_to_all | solution.py:602
  95.1 110.4 %copy-start.1 = (bf16[4,6,24,384]{3,2,1,0:T(8,128)(2,1)}, bf16[4,6,24,384]{3,2,1,0:T(8,128)(2,1)S(1)}, u32[]{:S(2)}) copy-start(bf16[4,6,24,384]{3,2,1,0:T(8,128)(2,1)S(1)} %get-tuple-element.23.refs_0_.rho_ref) | copy-start | bytes 1327108
  95.1 116.3 %copy-start.5 = (bf16[4,6,24,384]{3,2,1,0:T(8,128)(2,1)}, bf16[4,6,24,384]{3,2,1,0:T(8,128)(2,1)S(1)}, u32[]{:S(2)}) copy-start(bf16[4,6,24,384]{3,2,1,0:T(8,128)(2,1)S(1)} %get-tuple-element.22.gy_ref) | copy-start | bytes 1327108
  95.1 38.3 %collective-permute-start = (bf16[4,6,24,384]{3,2,1,0:T(8,128)(2,1)S(1)}, bf16[4,6,24,384]{3,2,1,0:T(8,128)(2,1)S(1)}, u32[]{:S(2)}, u32[]{:S(2)}) collective-permute-start(bf16[4,6,24,384]{3,2,1,0:T(8,128)(2,1)S(1)} %get-tuple-element.23.refs_0_.rho_ref), channel_id=1, source_target_pairs={{0,24},{8,0},{16,8},{24,16},{1,25},{9,1},{17,9},{25,17},{2,26},{10... | collective-permute-start | bytes 1327112 | tf_op jit(solution)/shard_map/ppermute | solution.py:455
  117.1 16.4 %all-to-all-start.5 = ((bf16[4,6,24,384]{3,2,1,0:T(8,128)(2,1)}), bf16[4,6,24,384]{3,2,1,0:T(8,128)(2,1)S(1)}, u32[]{:S(2)}, u32[]{:S(2)}) async-start(bf16[4,6,24,384]{3,2,1,0:T(8,128)(2,1)} %hartree.1), calls=%async_computation.5 | async-start | bytes 884736 | tf_op jit(solution)/shard_map/all_to_all | solution.py:615
  120.5 21.3 %collective-permute-start.4 = (bf16[4,6,24,384]{3,2,1,0:T(8,128)(2,1)S(1)}, bf16[4,6,24,384]{3,2,1,0:T(8,128)(2,1)S(1)}, u32[]{:S(2)}, u32[]{:S(2)}) collective-permute-start(bf16[4,6,24,384]{3,2,1,0:T(8,128)(2,1)S(1)} %get-tuple-element.23.refs_0_.rho_ref), channel_id=1, source_target_pairs={{0,8},{8,16},{16,24},{24,0},{1,9},{9,17},{17,25},{25,1},{2,10},{10... | collective-permute-start | bytes 1327112 | tf_op jit(solution)/shard_map/ppermute | solution.py:454
  128.0 16.2 %collective-permute-start.6 = (bf16[4,6,24,384]{3,2,1,0:T(8,128)(2,1)S(1)}, bf16[4,6,24,384]{3,2,1,0:T(8,128)(2,1)}, u32[]{:S(2)}, u32[]{:S(2)}) collective-permute-start(bf16[4,6,24,384]{3,2,1,0:T(8,128)(2,1)S(1)} %get-tuple-element.23.refs_0_.rho_ref), channel_id=1, source_target_pairs={{0,1},{1,0},{2,3},{3,2},{4,5},{5,4},{6,7},{7,6},{8,9},{9,8},{10,11... | collective-permute-start | bytes 1327112 | tf_op jit(solution)/shard_map/ppermute | solution.py:589
  129.6 21.7 %collective-permute-start.13 = (bf16[4,6,24,384]{3,2,1,0:T(8,128)(2,1)S(1)}, bf16[4,6,24,384]{3,2,1,0:T(8,128)(2,1)S(1)}, u32[]{:S(2)}, u32[]{:S(2)}) collective-permute-start(bf16[4,6,24,384]{3,2,1,0:T(8,128)(2,1)S(1)} %get-tuple-element.22.gy_ref), channel_id=1, source_target_pairs={{0,8},{8,16},{16,24},{24,0},{1,9},{9,17},{17,25},{25,1},{2,10},{10... | collective-permute-start | bytes 1327112 | tf_op jit(solution)/shard_map/ppermute | solution.py:454
  132.4 30.7 %collective-permute-start.2 = (bf16[4,6,24,384]{3,2,1,0:T(8,128)(2,1)S(1)}, bf16[4,6,24,384]{3,2,1,0:T(8,128)(2,1)S(1)}, u32[]{:S(2)}, u32[]{:S(2)}) collective-permute-start(bf16[4,6,24,384]{3,2,1,0:T(8,128)(2,1)S(1)} %get-tuple-element.22.gy_ref), channel_id=1, source_target_pairs={{0,24},{8,0},{16,8},{24,16},{1,25},{9,1},{17,9},{25,17},{2,26},{10... | collective-permute-start | bytes 1327112 | tf_op jit(solution)/shard_map/ppermute | solution.py:455
  133.5 48.3 %collective-permute-start.15 = (bf16[4,6,24,384]{3,2,1,0:T(8,128)(2,1)S(1)}, bf16[4,6,24,384]{3,2,1,0:T(8,128)(2,1)S(1)}, u32[]{:S(2)}, u32[]{:S(2)}) collective-permute-start(bf16[4,6,24,384]{3,2,1,0:T(8,128)(2,1)S(1)} %all-to-all-done.5.hartree_ref), channel_id=1, source_target_pairs={{0,8},{8,16},{16,24},{24,0},{1,9},{9,17},{17,25},{25,1},{2,10},{10... | collective-permute-start | bytes 1327112 | tf_op jit(solution)/shard_map/ppermute | solution.py:454
  141.8 33.3 %collective-permute-start.1 = (bf16[2,6,24,384]{3,2,1,0:T(8,128)(2,1)S(1)}, bf16[2,6,24,384]{3,2,1,0:T(8,128)(2,1)S(1)}, u32[]{:S(2)}, u32[]{:S(2)}) collective-permute-start(bf16[2,6,24,384]{3,2,1,0:T(8,128)(2,1)S(1)} %slice.58), channel_id=1, source_target_pairs={{0,24},{8,0},{16,8},{24,16},{1,25},{9,1},{17,9},{25,17},{2,26},{10... | collective-permute-start | bytes 663560 | tf_op jit(solution)/shard_map/ppermute | solution.py:452
  144.2 35.7 %collective-permute-start.5 = (bf16[2,6,24,384]{3,2,1,0:T(8,128)(2,1)S(1)}, bf16[2,6,24,384]{3,2,1,0:T(8,128)(2,1)S(1)}, u32[]{:S(2)}, u32[]{:S(2)}) collective-permute-start(bf16[2,6,24,384]{3,2,1,0:T(8,128)(2,1)S(1)} %slice.61), channel_id=1, source_target_pairs={{0,8},{8,16},{16,24},{24,0},{1,9},{9,17},{17,25},{25,1},{2,10},{10... | collective-permute-start | bytes 663560 | tf_op jit(solution)/shard_map/ppermute | solution.py:451
  151.3 46.6 %collective-permute-start.11 = (bf16[4,6,24,384]{3,2,1,0:T(8,128)(2,1)S(1)}, bf16[4,6,24,384]{3,2,1,0:T(8,128)(2,1)S(1)}, u32[]{:S(2)}, u32[]{:S(2)}) collective-permute-start(bf16[4,6,24,384]{3,2,1,0:T(8,128)(2,1)S(1)} %all-to-all-done.5.hartree_ref), channel_id=1, source_target_pairs={{0,24},{8,0},{16,8},{24,16},{1,25},{9,1},{17,9},{25,17},{2,26},{10... | collective-permute-start | bytes 1327112 | tf_op jit(solution)/shard_map/ppermute | solution.py:455
  163.1 40.1 %collective-permute-start.7 = (bf16[4,6,24,384]{3,2,1,0:T(8,128)(2,1)S(1)}, bf16[4,6,24,384]{3,2,1,0:T(8,128)(2,1)S(1)}, u32[]{:S(2)}, u32[]{:S(2)}) collective-permute-start(bf16[4,6,24,384]{3,2,1,0:T(8,128)(2,1)S(1)} %collective-permute-done.4.refs_1_.rho_ref), channel_id=1, source_target_pairs={{0,1},{1,0},{2,3},{3,2},{4,5},{5,4},{6,7},{7,6},{8,9},{9,8},{10,11... | collective-permute-start | bytes 1327112 | tf_op jit(solution)/shard_map/ppermute | solution.py:589
  175.2 30.3 %collective-permute-start.8 = (bf16[4,6,24,384]{3,2,1,0:T(8,128)(2,1)S(1)}, bf16[4,6,24,384]{3,2,1,0:T(8,128)(2,1)}, u32[]{:S(2)}, u32[]{:S(2)}) collective-permute-start(bf16[4,6,24,384]{3,2,1,0:T(8,128)(2,1)S(1)} %collective-permute-done.refs_2_.rho_ref), channel_id=1, source_target_pairs={{0,1},{1,0},{2,3},{3,2},{4,5},{5,4},{6,7},{7,6},{8,9},{9,8},{10,11... | collective-permute-start | bytes 1327112 | tf_op jit(solution)/shard_map/ppermute | solution.py:589
  179.8 13.1 %collective-permute-start.10 = (bf16[2,6,24,384]{3,2,1,0:T(8,128)(2,1)S(1)}, bf16[2,6,24,384]{3,2,1,0:T(8,128)(2,1)S(1)}, u32[]{:S(2)}, u32[]{:S(2)}) collective-permute-start(bf16[2,6,24,384]{3,2,1,0:T(8,128)(2,1)S(1)} %collective-permute-done.1.refs_4_.rho_ref), channel_id=1, source_target_pairs={{0,1},{1,0},{2,3},{3,2},{4,5},{5,4},{6,7},{7,6},{8,9},{9,8},{10,11... | collective-permute-start | bytes 663560 | tf_op jit(solution)/shard_map/ppermute | solution.py:589
  181.8 20.1 %collective-permute-start.9 = (bf16[2,6,24,384]{3,2,1,0:T(8,128)(2,1)S(1)}, bf16[2,6,24,384]{3,2,1,0:T(8,128)(2,1)S(1)}, u32[]{:S(2)}, u32[]{:S(2)}) collective-permute-start(bf16[2,6,24,384]{3,2,1,0:T(8,128)(2,1)S(1)} %collective-permute-done.5.refs_3_.rho_ref), channel_id=1, source_target_pairs={{0,1},{1,0},{2,3},{3,2},{4,5},{5,4},{6,7},{7,6},{8,9},{9,8},{10,11... | collective-permute-start | bytes 663560 | tf_op jit(solution)/shard_map/ppermute | solution.py:589
  193.0 35.0 %collective-permute-start.14 = (bf16[2,6,24,384]{3,2,1,0:T(8,128)(2,1)}, bf16[2,6,24,384]{3,2,1,0:T(8,128)(2,1)}, u32[]{:S(2)}, u32[]{:S(2)}) collective-permute-start(bf16[2,6,24,384]{3,2,1,0:T(8,128)(2,1)} %slice.63), channel_id=1, source_target_pairs={{0,8},{8,16},{16,24},{24,0},{1,9},{9,17},{17,25},{25,1},{2,10},{10... | collective-permute-start | bytes 663560 | tf_op jit(solution)/shard_map/ppermute | solution.py:451
  197.9 30.1 %collective-permute-start.16 = (bf16[2,6,24,384]{3,2,1,0:T(8,128)(2,1)}, bf16[2,6,24,384]{3,2,1,0:T(8,128)(2,1)}, u32[]{:S(2)}, u32[]{:S(2)}) collective-permute-start(bf16[2,6,24,384]{3,2,1,0:T(8,128)(2,1)} %slice.64), channel_id=1, source_target_pairs={{0,8},{8,16},{16,24},{24,0},{1,9},{9,17},{17,25},{25,1},{2,10},{10... | collective-permute-start | bytes 663560 | tf_op jit(solution)/shard_map/ppermute | solution.py:451
  201.9 29.5 %collective-permute-start.3 = (bf16[2,6,24,384]{3,2,1,0:T(8,128)(2,1)}, bf16[2,6,24,384]{3,2,1,0:T(8,128)(2,1)S(1)}, u32[]{:S(2)}, u32[]{:S(2)}) collective-permute-start(bf16[2,6,24,384]{3,2,1,0:T(8,128)(2,1)} %slice.60), channel_id=1, source_target_pairs={{0,24},{8,0},{16,8},{24,16},{1,25},{9,1},{17,9},{25,17},{2,26},{10... | collective-permute-start | bytes 663560 | tf_op jit(solution)/shard_map/ppermute | solution.py:452
  204.0 27.4 %collective-permute-start.12 = (bf16[2,6,24,384]{3,2,1,0:T(8,128)(2,1)}, bf16[2,6,24,384]{3,2,1,0:T(8,128)(2,1)}, u32[]{:S(2)}, u32[]{:S(2)}) collective-permute-start(bf16[2,6,24,384]{3,2,1,0:T(8,128)(2,1)} %slice.62), channel_id=1, source_target_pairs={{0,24},{8,0},{16,8},{24,16},{1,25},{9,1},{17,9},{25,17},{2,26},{10... | collective-permute-start | bytes 663560 | tf_op jit(solution)/shard_map/ppermute | solution.py:452
  (16 other events, 432.1 us)
